TPU v7x, 16 devices: a 4x2x1 block of a 4x4x8 slice. The times are simulated.
16 devices in a mesh: dp: 2 (over y, z), tp: 8 (over x, core).
Axes of the slice: x: 4, y: 2, z: 1, core: 2. Of those that a mesh axis runs over, the one named last changes fastest.
The devices are a block of a 4x4x8 slice.
Arguments:
- x: bfloat16 [4096, 4096], P('dp'), parts along dimension 0
- mu1: float32 [4096], P('dp'), parts along dimension 0
- rs1: float32 [4096], P('dp'), parts along dimension 0
- g1: bfloat16 [4096], replicated
- g2: bfloat16 [4096], replicated
- dy: bfloat16 [4096, 4096], P('dp'), parts along dimension 0
- wqkv: bfloat16 [4096, 12288], P(None, 'tp')
- wo: bfloat16 [32, 128, 4096], P('tp')
- w1: bfloat16 [4096, 16384], P(None, 'tp')
- w2: bfloat16 [16384, 4096], P('tp')
Outputs:
- output 1: bfloat16 [4096, 4096], P('dp'), parts along dimension 0
- output 2: bfloat16 [8192, 12288], P('dp', 'tp'), parts along dimension 0
- output 3: bfloat16 [64, 128, 4096], P(('dp', 'tp')), parts along dimension 0
- output 4: bfloat16 [8192, 16384], P('dp', 'tp'), parts along dimension 0
- output 5: bfloat16 [32768, 4096], P(('dp', 'tp')), parts along dimension 0
There are 2 independent parts. A program takes and returns all parts, laid end to end along the dimension named above; an argument that names none is the same for every part.
All inputs are finite; a program needn't handle non-finite values.
Results may differ from a plain program's by a relative error of at most 0.016693.
Values are sent between devices in bfloat16 or wider.
A program may use at most 768 MiB of HBM per device.

v0:
```python
import jax
import jax.numpy as jnp
from jax import lax
from jax.sharding import PartitionSpec as P

EPS = 1.0 / 100000


def _ln_bwd(dn, xh, rs, g):
    u = dn * g
    return rs[..., None] * (u - jnp.mean(u, axis=-1, keepdims=True) - xh * jnp.mean(u * xh, axis=-1, keepdims=True))


def _probs(q, k):
    n = q.shape[0]
    s = jnp.dot(q, k.T, preferred_element_type=jnp.float32) * q.shape[1] ** -0.5
    mask = jnp.arange(n)[:, None] >= jnp.arange(n)[None, :]
    return jax.nn.softmax(jnp.where(mask, s, -jnp.inf), axis=-1)


def _head_fwd(qkv):
    q, k, v = qkv[:, 0], qkv[:, 1], qkv[:, 2]
    p = _probs(q, k)
    return jnp.dot(p.astype(jnp.bfloat16), v, preferred_element_type=jnp.float32).astype(jnp.bfloat16)


def _head_bwd(args):
    qkv, do = args
    q, k, v = qkv[:, 0], qkv[:, 1], qkv[:, 2]
    p = _probs(q, k)
    dv = jnp.dot(p.astype(jnp.bfloat16).T, do, preferred_element_type=jnp.float32)
    dpm = jnp.dot(do, v.T, preferred_element_type=jnp.float32)
    ds = (p * (dpm - jnp.sum(p * dpm, axis=-1, keepdims=True)) * q.shape[1] ** -0.5).astype(jnp.bfloat16)
    dq = jnp.dot(ds, k, preferred_element_type=jnp.float32)
    dk = jnp.dot(ds.T, q, preferred_element_type=jnp.float32)
    return jnp.stack([dq, dk, dv], axis=1).astype(jnp.bfloat16)


def solution(mesh):
    def body(x, mu1, rs1, g1, g2, dy, wqkv, wo, w1, w2):
        f32 = jnp.float32
        bf = jnp.bfloat16
        hl, hd, d = wo.shape
        t = x.shape[0]
        xf = x.astype(f32)
        g1f = g1.astype(f32)
        g2f = g2.astype(f32)
        xh1 = (xf - mu1[:, None]) * rs1[:, None]
        n1 = (xh1 * g1f).astype(bf)
        qkv = jnp.dot(n1, wqkv, preferred_element_type=f32).astype(bf)
        qkv = jnp.moveaxis(qkv.reshape(t, hl, 3, hd), 1, 0)
        o = lax.map(_head_fwd, qkv)
        o = jnp.moveaxis(o, 0, 1).reshape(t, hl * hd)
        wo2 = wo.reshape(hl * hd, d)
        attn = jnp.dot(o, wo2, preferred_element_type=f32).astype(bf)
        h1 = xf + lax.psum(attn, "tp").astype(f32)
        mu2 = jnp.mean(h1, axis=-1, keepdims=True)
        xc = h1 - mu2
        rs2 = lax.rsqrt(jnp.mean(xc * xc, axis=-1) + EPS)
        xh2 = xc * rs2[:, None]
        n2 = (xh2 * g2f).astype(bf)
        a = jnp.dot(n2, w1, preferred_element_type=f32)
        gl, gelu_vjp = jax.vjp(jax.nn.gelu, a)
        gb = gl.astype(bf)
        dw2 = jnp.dot(gb.T, dy, preferred_element_type=f32).astype(bf)
        dg = jnp.dot(dy, w2.T, preferred_element_type=f32)
        da = gelu_vjp(dg)[0].astype(bf)
        dw1 = jnp.dot(n2.T, da, preferred_element_type=f32).astype(bf)
        dn2 = jnp.dot(da, w1.T, preferred_element_type=f32).astype(bf)
        dn2 = lax.psum(dn2, "tp").astype(f32)
        dh1 = dy.astype(f32) + _ln_bwd(dn2, xh2, rs2, g2f)
        dh1b = dh1.astype(bf)
        dwo = jnp.dot(o.T, dh1b, preferred_element_type=f32).astype(bf).reshape(hl, hd, d)
        do = jnp.dot(dh1b, wo2.T, preferred_element_type=f32).astype(bf)
        do = jnp.moveaxis(do.reshape(t, hl, hd), 1, 0)
        dqkv = lax.map(_head_bwd, (qkv, do))
        dqkv = jnp.moveaxis(dqkv, 0, 1).reshape(t, 3 * hl * hd)
        dwqkv = jnp.dot(n1.T, dqkv, preferred_element_type=f32).astype(bf)
        dn1 = jnp.dot(dqkv, wqkv.T, preferred_element_type=f32).astype(bf)
        dn1 = lax.psum(dn1, "tp").astype(f32)
        dx = (dh1 + _ln_bwd(dn1, xh1, rs1, g1f)).astype(bf)
        return dx, dwqkv, dwo, dw1, dw2

    return jax.shard_map(
        body, mesh=mesh,
        in_specs=(P("dp", None), P("dp"), P("dp"), P(None), P(None), P("dp", None),
                  P(None, "tp"), P("tp", None, None), P(None, "tp"), P("tp", None)),
        out_specs=(P("dp", None), P("dp", "tp"), P(("dp", "tp"), None, None), P("dp", "tp"), P(("dp", "tp"), None)),
        check_vma=False)
```

profile of v0, /device:TPU:113, one launch (start us, length us, event | category | flops | bytes accessed | tf_op | source)
XLA Modules:
  0.0 1155.0 jit_solution(12488441386678220180)
XLA Ops:
  8.0 35.5 %convolution_convert_fusion.7 = bf16[2048,1536]{0,1:T(8,128)(2,1)} fusion(bf16[4096,1536]{1,0:T(8,128)(2,1)} %param.20, bf16[2048,4096]{1,0:T(8,128)(2,1)} %param.14, f32[4096]{0:T(1024)S(1)} %convert_element_type.88, f32[2048]{0:T(1024)} %param.16, f32[2048]{0:T(1024)} %param.15), kind=kOutput, calls=%fused_computation.94 | convolution fusion | flops 25814892544 | bytes 35684352 | tf_op jit(solution)/shard_map/dot_general | solution.py:50
  43.5 8.6 copy.17
  52.1 60.7 %while.20 = (s32[]{:T(128)}, bf16[4,2048,128]{2,1,0:T(8,128)(2,1)S(1)}, bf16[4,2048,3,128]{3,1,2,0:T(8,128)(2,1)}, s32[]{:T(128)}) while((s32[]{:T(128)}, bf16[4,2048,128]{2,1,0:T(8,128)(2,1)S(1)}, bf16[4,2048,3,128]{3,1,2,0:T(8,128)(2,1)}, s32[]{:T(128)}) %tuple.60), condition=%wide.region_3.4_spmd, body=%wide.region_0.3_spmd.sunk | while | flops 2210656256 | bytes 55615556 | solution.py:52
  56.5 4.7 fusion.106
  61.1 6.5 fusion.107
  71.5 4.7 fusion.106
  76.2 6.5 fusion.107
  86.6 4.7 fusion.106
  91.3 6.5 fusion.107
  101.7 4.7 fusion.106
  106.3 6.5 fusion.107
  112.9 13.7 %bitcast_convert_fusion = bf16[2048,4096]{1,0:T(8,128)(2,1)} fusion(bf16[4,128,4096]{2,1,0:T(8,128)(2,1)} %param.21, bf16[4,2048,128]{2,1,0:T(8,128)(2,1)S(1)} %get-tuple-element.44), kind=kOutput, calls=%fused_computation.59 | convolution fusion | flops 8598323200 | bytes 23068672 | tf_op jit(solution)/shard_map/dot_general | solution.py:55
  129.6 43.2 %fusion.74 = f32[2048,2048]{1,0:T(8,128)} fusion(bf16[2048,4096]{1,0:T(8,128)(2,1)} %param.19, bf16[2048,4096]{1,0:T(8,128)(2,1)} %param.23), kind=kOutput, calls=%fused_computation.108 | convolution fusion | flops 34359738368 | bytes 50331648 | tf_op jit(solution)/shard_map/dot_general | solution.py:66
  172.8 131.0 %all-reduce.4.cloned.1.call-done = bf16[2048,4096]{1,0:T(8,128)(2,1)} async-done(((bf16[2048,4096]{1,0:T(8,128)(2,1)}), bf16[2048,4096]{1,0:T(8,128)(2,1)}) %all-reduce.4.cloned.1.call-update) | async-done | bytes 16777232 | tf_op jit(solution)/shard_map/psum | solution.py:56
  303.8 15.5 %fusion.44 = f32[2048]{0:T(1024)S(1)} fusion(bf16[2048,4096]{1,0:T(8,128)(2,1)} %all-reduce.4.cloned.1.call-done, bf16[2048,4096]{1,0:T(8,128)(2,1)} %param.14), kind=kLoop, calls=%fused_computation.69 | loop fusion | flops 33552384 | bytes 33562624 | tf_op jit(solution)/shard_map/reduce_sum | solution.py:57
  319.4 14.0 %multiply_reduce_fusion.2 = f32[2048]{0:T(1024)S(1)} fusion(bf16[2048,4096]{1,0:T(8,128)(2,1)S(1)} %copy-done, bf16[2048,4096]{1,0:T(8,128)(2,1)} %param.14, f32[2048]{0:T(1024)S(1)} %broadcast_multiply_fusion.4), kind=kLoop, calls=%fused_computation.67 | loop fusion | flops 50329600 | bytes 33570816 | tf_op jit(solution)/shard_map/reduce_sum | solution.py:59
  334.0 11.9 %multiply_convert_fusion.1 = bf16[2048,4096]{1,0:T(8,128)(2,1)} fusion(bf16[2048,4096]{1,0:T(8,128)(2,1)S(1)} %copy-done, bf16[2048,4096]{1,0:T(8,128)(2,1)S(1)} %bitcast.123, f32[4096]{0:T(1024)S(1)} %convert_element_type.93, f32[2048]{0:T(1024)S(1)} %add_rsqrt_fusion, f32[2048]{0:T(1024)S(1)} %broadcast_multiply_fusion.4), kind=kLoop, calls=%fused_computation.66 | loop fusion | flops 58720256 | bytes 50364416 | tf_op jit(solution)/shard_map/convert_element_type | solution.py:61
  345.9 56.5 %fusion.52 = (bf16[2048,2048]{1,0:T(8,128)(2,1)}, f32[2048,2048]{1,0:T(8,128)}) fusion(f32[2048,2048]{1,0:T(8,128)} %fusion.74, bf16[2048,4096]{1,0:T(8,128)(2,1)} %multiply_convert_fusion.1, bf16[4096,2048]{1,0:T(8,128)(2,1)} %param.22), kind=kOutput, calls=%fused_computation.79 | convolution fusion | flops 34443624448 | bytes 75497472 | tf_op jit(solution)/shard_map/dot_general | solution.py:62
  402.4 42.6 %convolution_convert_fusion.4 = bf16[4096,2048]{1,0:T(8,128)(2,1)} fusion(bf16[2048,4096]{1,0:T(8,128)(2,1)} %multiply_convert_fusion.1, bf16[2048,2048]{1,0:T(8,128)(2,1)} %get-tuple-element.70), kind=kOutput, calls=%fused_computation.83 | convolution fusion | flops 34368126976 | bytes 41943040 | tf_op jit(solution)/shard_map/dot_general | solution.py:68
  445.0 38.7 %convolution_convert_fusion.6 = bf16[2048,4096]{1,0:T(8,128)(2,1)} fusion(bf16[2048,2048]{1,0:T(8,128)(2,1)S(1)} %copy-done.14, bf16[4096,2048]{1,0:T(8,128)(2,1)S(1)} %copy-done.13), kind=kOutput, calls=%fused_computation.85 | convolution fusion | flops 34368126976 | bytes 41943040 | tf_op jit(solution)/shard_map/dot_general | solution.py:69
  483.8 48.4 %convolution_convert_fusion.3 = bf16[2048,4096]{1,0:T(8,128)(2,1)} fusion(bf16[2048,4096]{1,0:T(8,128)(2,1)} %param.19, f32[2048,2048]{1,0:T(8,128)} %get-tuple-element.71), kind=kOutput, calls=%fused_computation.82 | convolution fusion | flops 34405875712 | bytes 50331648 | tf_op jit(solution)/shard_map/dot_general | solution.py:65
  532.2 126.3 %all-reduce.6.cloned.1.call-done = bf16[2048,4096]{1,0:T(8,128)(2,1)} async-done(((bf16[2048,4096]{1,0:T(8,128)(2,1)}), bf16[2048,4096]{1,0:T(8,128)(2,1)}) %all-reduce.6.cloned.1.call-update) | async-done | bytes 16777232 | tf_op jit(solution)/shard_map/psum | solution.py:70
  658.6 20.1 %fusion.42 = (f32[2048]{0:T(1024)S(1)}, f32[2048]{0:T(1024)S(1)}) fusion(bf16[2048,4096]{1,0:T(8,128)(2,1)} %all-reduce.6.cloned.1.call-done, f32[4096]{0:T(1024)S(1)} %copy-done.3, f32[2048]{0:T(1024)S(1)} %copy-done.9, f32[2048]{0:T(1024)S(1)} %copy-done.5, bf16[2048,4096]{1,0:T(8,128)(2,1)} %all-reduce.4.cloned.1.call-done, bf16[2048,4096]{1,0:T(8,128)(2,1)} %param.14), kind=kLoop, calls=%fused_computation.65 | loop fusion | flops 83881984 | bytes 50380800 | tf_op jit(solution)/shard_map/reduce_sum | solution.py:11
  678.7 33.8 %multiply_add_fusion = f32[2048,4096]{1,0:T(8,128)} fusion(bf16[2048,4096]{1,0:T(8,128)(2,1)} %all-reduce.6.cloned.1.call-done, bf16[2048,4096]{1,0:T(8,128)(2,1)} %param.19, bf16[2048,4096]{1,0:T(8,128)(2,1)} %all-reduce.4.cloned.1.call-done, bf16[2048,4096]{1,0:T(8,128)(2,1)} %param.14, f32[2048]{0:T(1024)S(1)} %get-tuple-element.72, ...), kind=kLoop, calls=%fused_computation.62 | loop fusion | flops 109051904 | bytes 100712448 | tf_op jit(solution)/shard_map/add | solution.py:71
  712.5 16.3 %fusion.64 = bf16[2048,512]{0,1:T(8,128)(2,1)S(1)} fusion(bf16[512,4096]{1,0:T(8,128)(2,1)} %bitcast.131, f32[2048,4096]{1,0:T(8,128)} %multiply_add_fusion), kind=kOutput, calls=%fused_computation.96 | convolution fusion | flops 8599371776 | bytes 39845888 | tf_op jit(solution)/shard_map/dot_general | solution.py:74
  731.3 164.8 %while.21 = (s32[]{:T(128)}, bf16[4,2048,3,128]{1,3,2,0:T(8,128)(2,1)}, bf16[4,2048,3,128]{3,1,2,0:T(8,128)(2,1)}, bf16[4,2048,128]{2,1,0:T(8,128)(2,1)}, s32[]{:T(128)}) while((s32[]{:T(128)}, bf16[4,2048,3,128]{1,3,2,0:T(8,128)(2,1)}, bf16[4,2048,3,128]{3,1,2,0:T(8,128)(2,1)}, bf16[4,2048,128]{2,1,0:T(8,128)(2,1)}, s32[]{:T(128)}) %tuple.62), condition=%wide.region_14.15_spmd, body=%wide.region_10.14_spmd.sunk | while | flops 5501085696 | bytes 160522320 | solution.py:76
  735.6 4.7 fusion.113
  740.3 5.9 fusion.114
  746.1 10.1 multiply_reduce_fusion.4
  756.2 9.5 multiply_convert_fusion.5
  776.6 4.7 fusion.113
  781.3 5.9 fusion.114
  787.2 10.1 multiply_reduce_fusion.4
  797.2 9.5 multiply_convert_fusion.5
  817.7 4.7 fusion.113
  822.4 5.9 fusion.114
  828.3 10.1 multiply_reduce_fusion.4
  838.3 9.5 multiply_convert_fusion.5
  858.8 4.7 fusion.113
  863.4 5.9 fusion.114
  869.3 10.1 multiply_reduce_fusion.4
  879.4 9.5 multiply_convert_fusion.5
  896.1 33.0 %convolution_convert_fusion.5 = bf16[2048,4096]{1,0:T(8,128)(2,1)} fusion(bf16[2048,1536]{0,1:T(8,128)(2,1)} %bitcast.129, bf16[4096,1536]{1,0:T(8,128)(2,1)} %param.20), kind=kOutput, calls=%fused_computation.84 | convolution fusion | flops 25778192384 | bytes 35651584 | tf_op jit(solution)/shard_map/dot_general | solution.py:79
  930.7 16.4 %fusion.61 = bf16[512,4096]{1,0:T(8,128)(2,1)} fusion(bf16[2048,512]{0,1:T(8,128)(2,1)S(1)} %bitcast.126, f32[2048,4096]{1,0:T(8,128)} %multiply_add_fusion), kind=kOutput, calls=%fused_computation.95 | convolution fusion | flops 8600420352 | bytes 39845888 | tf_op jit(solution)/shard_map/dot_general | solution.py:73
  947.1 35.3 %convolution_convert_fusion.2 = bf16[4096,1536]{1,0:T(8,128)(2,1)} fusion(bf16[2048,1536]{0,1:T(8,128)(2,1)} %bitcast.130, bf16[2048,4096]{1,0:T(8,128)(2,1)} %param.14, f32[4096]{0:T(1024)S(1)} %copy-done.7, f32[2048]{0:T(1024)S(1)} %copy-done.10, f32[2048]{0:T(1024)S(1)} %copy-done.11), kind=kOutput, calls=%fused_computation.81 | convolution fusion | flops 25818038272 | bytes 35684352 | tf_op jit(solution)/shard_map/dot_general | solution.py:78
  982.5 121.6 %all-reduce.8.cloned.1.call-done = bf16[2048,4096]{1,0:T(8,128)(2,1)} async-done(((bf16[2048,4096]{1,0:T(8,128)(2,1)}), bf16[2048,4096]{1,0:T(8,128)(2,1)}) %all-reduce.8.cloned.1.call-update) | async-done | bytes 16777232 | tf_op jit(solution)/shard_map/psum | solution.py:80
  1104.1 15.8 %fusion.41 = (f32[2048]{0:T(1024)S(1)}, f32[2048]{0:T(1024)S(1)}) fusion(bf16[2048,4096]{1,0:T(8,128)(2,1)} %all-reduce.8.cloned.1.call-done, f32[4096]{0:T(1024)S(1)} %copy-done.7, f32[2048]{0:T(1024)S(1)} %copy-done.10, f32[2048]{0:T(1024)S(1)} %copy-done.11, bf16[2048,4096]{1,0:T(8,128)(2,1)} %param.14), kind=kLoop, calls=%fused_computation.61 | loop fusion | flops 67104768 | bytes 33603584 | tf_op jit(solution)/shard_map/reduce_sum | solution.py:11
  1119.9 28.3 %fusion.40 = bf16[2048,4096]{1,0:T(8,128)(2,1)} fusion(f32[2048,4096]{1,0:T(8,128)} %multiply_add_fusion, bf16[2048,4096]{1,0:T(8,128)(2,1)} %param.14, bf16[2048,4096]{1,0:T(8,128)(2,1)} %all-reduce.8.cloned.1.call-done, f32[2048]{0:T(1024)S(1)} %broadcast_multiply_fusion, f32[2048]{0:T(1024)S(1)} %broadcast_multiply_fusion.1, f32[4096]{0:T(1024)S(1)} %copy-done.7, ...), kind=kLoop, calls=%fused_computation.58 | loop fusion | flops 92274688 | bytes 83935232 | tf_op jit(solution)/shard_map/convert_element_type | solution.py:81
  (92 shorter events, 67.6 us)
Async XLA Ops:
  7.2 296.6 %all-reduce.4.cloned.1.call-start = ((), (), s32[]{:S(2)}) async-start(), calls=%async_computation | async-start | bytes 33554432 | tf_op jit(solution)/shard_map/psum | solution.py:56
  8.0 35.5 %copy-start.6 = (f32[4096]{0:T(1024)}, f32[4096]{0:T(1024)S(1)}, u32[]{:S(2)}) copy-start(f32[4096]{0:T(1024)S(1)} %convert_element_type.88) | copy-start | bytes 49156
  126.5 3.0 copy-start.12
  126.6 532.0 %all-reduce.6.cloned.1.call-start = ((), (), s32[]{:S(2)}) async-start(), calls=%async_computation.1 | async-start | bytes 33554432 | tf_op jit(solution)/shard_map/psum | solution.py:70
  129.5 203.8 %copy-start.2 = (f32[4096]{0:T(1024)}, f32[4096]{0:T(1024)S(1)}, u32[]{:S(2)}) copy-start(f32[4096]{0:T(1024)S(1)} %convert_element_type.93) | copy-start | bytes 49156
  303.8 15.5 %copy-start = (bf16[2048,4096]{1,0:T(8,128)(2,1)S(1)}, bf16[2048,4096]{1,0:T(8,128)(2,1)}, u32[]{:S(2)}) copy-start(bf16[2048,4096]{1,0:T(8,128)(2,1)} %all-reduce.4.cloned.1.call-done) | copy-start | bytes 50331652
  303.8 30.2 %slice-start = ((s8[16777216]{0:T(1024)(128)(4,1)}), s8[4194304]{0:T(1024)(128)(4,1)S(1)}, s32[]{:S(2)}) async-start(s8[16777216]{0:T(1024)(128)(4,1)} %bitcast.122), calls=%async_computation.3 | async-start | bytes 8388608
  303.8 30.2 %slice-start.1 = ((s8[16777216]{0:T(1024)(128)(4,1)}), s8[4194304]{0:T(1024)(128)(4,1)S(1)}, s32[]{:S(2)}) async-start(s8[16777216]{0:T(1024)(128)(4,1)} %bitcast.122), calls=%async_computation.4 | async-start | bytes 8388608
  319.3 14.0 %copy-start.4 = (f32[2048]{0:T(1024)}, f32[2048]{0:T(1024)S(1)}, u32[]{:S(2)}) copy-start(f32[2048]{0:T(1024)S(1)} %broadcast_multiply_fusion.4) | copy-start | bytes 24580
  319.3 14.6 %slice-start.2 = ((s8[16777216]{0:T(1024)(128)(4,1)}), s8[4194304]{0:T(1024)(128)(4,1)S(1)}, s32[]{:S(2)}) async-start(s8[16777216]{0:T(1024)(128)(4,1)} %bitcast.122), calls=%async_computation.5 | async-start | bytes 8388608
  319.3 14.6 %slice-start.3 = ((s8[16777216]{0:T(1024)(128)(4,1)}), s8[4194304]{0:T(1024)(128)(4,1)S(1)}, s32[]{:S(2)}) async-start(s8[16777216]{0:T(1024)(128)(4,1)} %bitcast.122), calls=%async_computation.6 | async-start | bytes 8388608
  333.4 0.6 copy-start.8
  402.4 42.6 %copy-start.13 = (bf16[4096,2048]{1,0:T(8,128)(2,1)S(1)}, bf16[4096,2048]{1,0:T(8,128)(2,1)}, u32[]{:S(2)}) copy-start(bf16[4096,2048]{1,0:T(8,128)(2,1)} %param.22) | copy-start | bytes 50331652
  402.4 42.6 %copy-start.14 = (bf16[2048,2048]{1,0:T(8,128)(2,1)S(1)}, bf16[2048,2048]{1,0:T(8,128)(2,1)}, u32[]{:S(2)}) copy-start(bf16[2048,2048]{1,0:T(8,128)(2,1)} %get-tuple-element.70) | copy-start | bytes 25165828
  483.7 620.3 %all-reduce.8.cloned.1.call-start = ((), (), s32[]{:S(2)}) async-start(), calls=%async_computation.2 | async-start | bytes 33554432 | tf_op jit(solution)/shard_map/psum | solution.py:80
  483.8 174.8 %copy-start.3 = (f32[4096]{0:T(1024)S(1)}, f32[4096]{0:T(1024)}, u32[]{:S(2)}) copy-start(f32[4096]{0:T(1024)} %copy-done.2) | copy-start | bytes 49156
  483.8 174.8 %copy-start.5 = (f32[2048]{0:T(1024)S(1)}, f32[2048]{0:T(1024)}, u32[]{:S(2)}) copy-start(f32[2048]{0:T(1024)} %copy-done.4) | copy-start | bytes 24580
  483.8 174.8 %copy-start.9 = (f32[2048]{0:T(1024)S(1)}, f32[2048]{0:T(1024)}, u32[]{:S(2)}) copy-start(f32[2048]{0:T(1024)} %copy-done.8) | copy-start | bytes 24580
  929.1 1.6 copy-start.1
  930.7 16.4 %copy-start.7 = (f32[4096]{0:T(1024)S(1)}, f32[4096]{0:T(1024)}, u32[]{:S(2)}) copy-start(f32[4096]{0:T(1024)} %copy-done.6) | copy-start | bytes 49156
  930.7 16.4 %copy-start.10 = (f32[2048]{0:T(1024)S(1)}, f32[2048]{0:T(1024)}, u32[]{:S(2)}) copy-start(f32[2048]{0:T(1024)} %param.16) | copy-start | bytes 24580
  930.7 16.4 %copy-start.11 = (f32[2048]{0:T(1024)S(1)}, f32[2048]{0:T(1024)}, u32[]{:S(2)}) copy-start(f32[2048]{0:T(1024)} %param.15) | copy-start | bytes 24580
Sparse Core Ops, SparseCore 0:
  126.7 177.0 all-reduce.3
  483.9 174.6 all-reduce.5
  929.3 174.6 all-reduce.7
where the time goes:
time: 1160 us; the launch traced here: 1150 us
  matrix products  508 us (44%)
  waiting for transfers between devices  379 us (33%)
  other arithmetic  216 us (19%)
  local copies, waits for them, and re-layouts  36.2 us (3%)
  between operations  14.2 us (1%)
    psum x1, waiting for transfers between devices, body(): h1 = xf + lax.psum(attn, 'tp').astype(f32)  131 us
    psum x1, waiting for transfers between devices, body(): dn2 = lax.psum(dn2, 'tp').astype(f32)  126 us
    psum x1, waiting for transfers between devices, body(): dn1 = lax.psum(dn1, 'tp').astype(f32)  122 us
    dot_general x1, matrix products, body(): a = jnp.dot(n2, w1, preferred_element_type=f32)  56.5 us
    dot_general x1, matrix products, body(): dw2 = jnp.dot(gb.T, dy, preferred_element_type=f32).astype(bf)  48.4 us
    dot_general x1, matrix products, body(): dg = jnp.dot(dy, w2.T, preferred_element_type=f32)  43.2 us
    dot_general x1, matrix products, body(): dw1 = jnp.dot(n2.T, da, preferred_element_type=f32).astype(bf)  42.6 us
    dot_general x4, matrix products, _head_bwd(): dpm = jnp.dot(do, v.T, preferred_element_type=jnp.float32)  40.3 us
  transfers between devices with their start and end apart: 3, of which 3 were waited for; matrix products, arithmetic and copies ran while one was open for 13% of the time, Pallas kernels for 0%

commit v1 on v0

v1 whole, which is shorter than its diff:
```python
import functools

import jax
import jax.numpy as jnp
from jax import lax
from jax.experimental import pallas as pl
from jax.experimental.pallas import tpu as pltpu
from jax.sharding import PartitionSpec as P

EPS = 1.0 / 100000
F32 = jnp.float32
BF = jnp.bfloat16
NC = 2
BQ = 512


def _ln_bwd(dn, xh, rs, g):
    u = dn * g
    return rs * (u - jnp.mean(u, axis=-1, keepdims=True) - xh * jnp.mean(u * xh, axis=-1, keepdims=True))


def _nt(a, b):
    return lax.dot_general(a, b, (((1,), (1,)), ((), ())), preferred_element_type=F32)


def _tn(a, b):
    return lax.dot_general(a, b, (((0,), (0,)), ((), ())), preferred_element_type=F32)


def _nn(a, b):
    return jnp.dot(a, b, preferred_element_type=F32)


def _attn_fwd_kernel(chunk, *refs):
    qkv, o_ref = refs[:-1], refs[-1]
    hd = o_ref.shape[1]
    rows = o_ref.shape[0]
    scale = hd ** -0.5
    bq = min(BQ, rows)
    for b in range(rows // bq):
        q = qkv[chunk][b * bq:(b + 1) * bq, 0:hd]
        parts = [(c, rows) for c in range(chunk)] + [(chunk, (b + 1) * bq)]
        s = [_nt(q, qkv[c][0:n, hd:2 * hd]) for c, n in parts]
        n = (b + 1) * bq
        row = b * bq + lax.broadcasted_iota(jnp.int32, (bq, n), 0)
        col = lax.broadcasted_iota(jnp.int32, (bq, n), 1)
        s[-1] = jnp.where(row >= col, s[-1], -jnp.inf)
        m = functools.reduce(jnp.maximum, [jnp.max(x, axis=-1, keepdims=True) for x in s])
        p = [jnp.exp((x - m) * scale) for x in s]
        l = functools.reduce(jnp.add, [jnp.sum(x, axis=-1, keepdims=True) for x in p])
        inv = 1.0 / l
        o = None
        for x, (c, n) in zip(p, parts):
            t = _nn((x * inv).astype(BF), qkv[c][0:n, 2 * hd:3 * hd])
            o = t if o is None else o + t
        o_ref[b * bq:(b + 1) * bq, :] = o.astype(BF)


def _attn_fwd(chunk, qkvs, hl, hd):
    rows = qkvs[0].shape[0]
    pairs = rows * rows * chunk + rows * rows // 2
    return pl.pallas_call(
        functools.partial(_attn_fwd_kernel, chunk),
        grid=(hl,),
        in_specs=[pl.BlockSpec((rows, 3 * hd), lambda h: (0, h)) for _ in range(chunk + 1)],
        out_specs=pl.BlockSpec((rows, hd), lambda h: (0, h)),
        out_shape=jax.ShapeDtypeStruct((rows, hl * hd), BF),
        compiler_params=pltpu.CompilerParams(vmem_limit_bytes=60 * 2 ** 20),
        cost_estimate=pl.CostEstimate(flops=8 * hl * pairs * hd, bytes_accessed=rows * hl * hd * 8 * (chunk + 1), transcendentals=hl * pairs),
        name=f"attn_fwd_{chunk}",
    )(*qkvs[:chunk + 1])


def _attn_bwd_kernel(chunk, nc, *refs):
    qkv, refs = refs[:chunk + 1], refs[chunk + 1:]
    do_ref, refs = refs[0], refs[1:]
    late = chunk < nc - 1
    prev, refs = (refs[:2], refs[2:]) if late else (None, refs)
    out_ref, refs = refs[0], refs[1:]
    part = refs[:2 * chunk]
    acc_k, acc_v = refs[2 * chunk:]
    hd = do_ref.shape[1]
    rows = do_ref.shape[0]
    scale = hd ** -0.5
    bq = min(BQ, rows)
    for b in range(rows // bq):
        sl = slice(b * bq, (b + 1) * bq)
        q = qkv[chunk][sl, 0:hd]
        do = do_ref[sl, :]
        parts = [(c, rows) for c in range(chunk)] + [(chunk, (b + 1) * bq)]
        s = [_nt(qkv[c][0:n, hd:2 * hd], q) for c, n in parts]
        n = (b + 1) * bq
        key = lax.broadcasted_iota(jnp.int32, (n, bq), 0)
        qry = b * bq + lax.broadcasted_iota(jnp.int32, (n, bq), 1)
        s[-1] = jnp.where(qry >= key, s[-1], -jnp.inf)
        m = functools.reduce(jnp.maximum, [jnp.max(x, axis=0, keepdims=True) for x in s])
        p = [jnp.exp((x - m) * scale) for x in s]
        inv = 1.0 / functools.reduce(jnp.add, [jnp.sum(x, axis=0, keepdims=True) for x in p])
        p = [x * inv for x in p]
        dp = [_nt(qkv[c][0:n, 2 * hd:3 * hd], do) for c, n in parts]
        r = functools.reduce(jnp.add, [jnp.sum(x * y, axis=0, keepdims=True) for x, y in zip(p, dp)])
        dq = None
        for x, y, (c, n) in zip(p, dp, parts):
            ds = (x * (y - r) * scale).astype(BF)
            dv = _nn(x.astype(BF), do)
            dk = _nn(ds, q)
            t = _tn(ds, qkv[c][0:n, hd:2 * hd])
            dq = t if dq is None else dq + t
            if c == chunk:
                if b == 0:
                    acc_k[0:n, :] = prev[0][0:n, :] + dk if late else dk
                    acc_v[0:n, :] = prev[1][0:n, :] + dv if late else dv
                else:
                    lo = b * bq
                    acc_k[0:lo, :] = acc_k[0:lo, :] + dk[0:lo]
                    acc_v[0:lo, :] = acc_v[0:lo, :] + dv[0:lo]
                    acc_k[lo:n, :] = prev[0][lo:n, :] + dk[lo:n] if late else dk[lo:n]
                    acc_v[lo:n, :] = prev[1][lo:n, :] + dv[lo:n] if late else dv[lo:n]
            elif b == 0:
                part[2 * c][...] = dk
                part[2 * c + 1][...] = dv
            else:
                part[2 * c][...] = part[2 * c][...] + dk
                part[2 * c + 1][...] = part[2 * c + 1][...] + dv
        out_ref[sl, 0:hd] = dq.astype(BF)
    out_ref[:, hd:2 * hd] = acc_k[...].astype(BF)
    out_ref[:, 2 * hd:3 * hd] = acc_v[...].astype(BF)


def _attn_bwd(chunk, nc, qkvs, do, prev, hl, hd):
    rows = do.shape[0]
    pairs = rows * rows * chunk + rows * rows // 2
    wide = pl.BlockSpec((rows, 3 * hd), lambda h: (0, h))
    one = pl.BlockSpec((rows, hd), lambda h: (0, h))
    res = pl.pallas_call(
        functools.partial(_attn_bwd_kernel, chunk, nc),
        grid=(hl,),
        in_specs=[wide] * (chunk + 1) + [one] + [one] * len(prev),
        out_specs=[wide] + [one] * (2 * chunk),
        out_shape=[jax.ShapeDtypeStruct((rows, 3 * hl * hd), BF)]
        + [jax.ShapeDtypeStruct((rows, hl * hd), F32)] * (2 * chunk),
        scratch_shapes=[pltpu.VMEM((rows, hd), F32), pltpu.VMEM((rows, hd), F32)],
        compiler_params=pltpu.CompilerParams(vmem_limit_bytes=62 * 2 ** 20),
        cost_estimate=pl.CostEstimate(flops=20 * hl * pairs * hd, bytes_accessed=rows * hl * hd * 8 * (chunk + 2), transcendentals=hl * pairs),
        name=f"attn_bwd_{chunk}",
    )(*qkvs[:chunk + 1], do, *prev)
    return res[0], list(res[1:])


MESH = pl.DeviceIdType.MESH
VMEM = 62 * 2 ** 20
C0 = 0.7978845608028654
C1 = 0.044715


def _dot(a, b, ta, tb):
    return lax.dot_general(a, b, (((0 if ta else 1,), (1 if tb else 0,)), ((), ())), preferred_element_type=F32)


def _norm_qkv_kernel(x_ref, mu_ref, rs_ref, g_ref, w_ref, n_ref, o_ref):
    xh = (x_ref[...].astype(F32) - mu_ref[...]) * rs_ref[...]
    n_ref[...] = (xh * g_ref[...]).astype(BF)
    o_ref[...] = _nn(n_ref[...], w_ref[...]).astype(BF)


def _norm_qkv(x, mu, rs, g, w, lo, rows):
    bm = 256
    d, n = w.shape
    off = lo // bm
    return pl.pallas_call(
        _norm_qkv_kernel,
        grid=(rows // bm,),
        in_specs=[pl.BlockSpec((bm, d), lambda i: (i + off, 0)),
                  pl.BlockSpec((bm, 1), lambda i: (i + off, 0)),
                  pl.BlockSpec((bm, 1), lambda i: (i + off, 0)),
                  pl.BlockSpec((1, d), lambda i: (0, 0)),
                  pl.BlockSpec((d, n), lambda i: (0, 0))],
        out_specs=[pl.BlockSpec((bm, d), lambda i: (i, 0)), pl.BlockSpec((bm, n), lambda i: (i, 0))],
        out_shape=[jax.ShapeDtypeStruct((rows, d), BF), jax.ShapeDtypeStruct((rows, n), BF)],
        compiler_params=pltpu.CompilerParams(vmem_limit_bytes=VMEM),
        cost_estimate=pl.CostEstimate(flops=2 * rows * d * n, bytes_accessed=2 * (2 * rows * d + d * n + rows * n), transcendentals=0),
        name="norm_qkv",
    )(x, mu, rs, g, w)


def _gather_events(step, marks, shard, out, local, ssem, rsem):
    tp = lax.axis_size("tp")
    me = lax.axis_index("tp")
    chips = tp // 2
    chip, core = me // 2, lax.rem(me, 2)
    sr = shard.shape[0]
    h = sr // 2

    def dev(shift, other=0):
        k = 1 - core if other else core
        return lax.rem(chip + shift, chips) * 2 + k

    right, left, opp, mate = dev(1), dev(chips - 1), dev(2), dev(0, 1)

    def rows(owner, part=None):
        if part is None:
            return out.at[pl.ds(pl.multiple_of(owner * sr, 8), sr)]
        return out.at[pl.ds(pl.multiple_of(owner * sr + part * h, 8), h)]

    def copy(i, src, dst, to):
        return pltpu.make_async_remote_copy(src_ref=src, dst_ref=dst, send_sem=ssem.at[i], recv_sem=rsem.at[i],
                                            device_id={"tp": to}, device_id_type=MESH)

    lo, hi = shard.at[pl.ds(0, h)], shard.at[pl.ds(h, h)]
    sends = [copy(0, lo, rows(me, 0), right), copy(1, hi, rows(me, 1), left),
             copy(2, hi, rows(me, 1), right), copy(3, lo, rows(me, 0), left),
             copy(4, shard, rows(me), mate),
             copy(5, rows(left, 0), rows(left, 0), right), copy(6, rows(right, 1), rows(right, 1), left),
             copy(7, rows(left), rows(left), mate), copy(8, rows(right), rows(right), mate),
             copy(9, rows(opp), rows(opp), mate)]
    lands = [rows(left, 0), rows(right, 1), rows(left, 1), rows(right, 0), rows(mate), rows(opp, 0), rows(opp, 1),
             rows(dev(chips - 1, 1)), rows(dev(1, 1)), rows(dev(2, 1))]

    def landed(i):
        copy(i, lands[i], lands[i], mate).wait_recv()

    own = pltpu.make_async_copy(shard, rows(me), local)

    @pl.when(step == 0)
    def _():
        bar = pltpu.get_barrier_semaphore()
        for to in (left, right, mate):
            pl.semaphore_signal(bar, inc=1, device_id={"tp": to}, device_id_type=MESH)
        pl.semaphore_wait(bar, 3)
        for i in range(5):
            sends[i].start()
        own.start()

    @pl.when(step == marks[0])
    def _():
        landed(0)
        sends[5].start()
        landed(1)
        sends[6].start()

    @pl.when(step == marks[1])
    def _():
        landed(2)
        sends[7].start()
        landed(3)
        sends[8].start()

    def finish():
        landed(5)
        landed(6)
        sends[9].start()
        for i in (4, 7, 8, 9):
            landed(i)
        own.wait()
        for cp in sends:
            cp.wait_send()

    return finish


def _mm(body, grid, ins, in_specs, outs, out_specs, flops, name, shard=None, cid=0, marks=(0, 0)):
    n_in, n_out = len(ins), len(outs)
    steps = grid[0] * grid[1]

    def plain(*refs):
        body(refs[:n_in], refs[n_in:])

    def comm(*refs):
        sh, out = refs[n_in], refs[n_in + 1 + n_out]
        step = pl.program_id(0) * grid[1] + pl.program_id(1)
        finish = _gather_events(step, marks, sh, out, *refs[n_in + n_out + 2:])
        body(refs[:n_in], refs[n_in + 1:n_in + 1 + n_out])
        pl.when(step == steps - 1)(finish)

    nbytes = sum(v.size * v.dtype.itemsize for v in ins) + sum(v.size * v.dtype.itemsize for v in outs)
    cost = pl.CostEstimate(flops=flops, bytes_accessed=nbytes, transcendentals=0)
    if shard is None:
        return pl.pallas_call(plain, grid=grid, in_specs=in_specs, out_specs=out_specs, out_shape=outs, cost_estimate=cost,
                              compiler_params=pltpu.CompilerParams(vmem_limit_bytes=VMEM), name=name)(*ins)
    any_spec = pl.BlockSpec(memory_space=pl.ANY)
    full = jax.ShapeDtypeStruct((shard.shape[0] * lax.axis_size("tp"), shard.shape[1]), shard.dtype)
    return pl.pallas_call(
        comm, grid=grid, in_specs=in_specs + [any_spec], out_specs=out_specs + [any_spec], out_shape=outs + [full],
        scratch_shapes=[pltpu.SemaphoreType.DMA, pltpu.SemaphoreType.DMA((10,)), pltpu.SemaphoreType.DMA((10,))],
        cost_estimate=cost, name=name,
        compiler_params=pltpu.CompilerParams(vmem_limit_bytes=VMEM, collective_id=cid, has_side_effects=True))(*ins, shard)


def _matmul(a, b, tb, bm, bn, name, dtype=BF, **kw):
    m, k = a.shape
    n = b.shape[0] if tb else b.shape[1]

    def body(i, o):
        o[0][...] = _dot(i[0][...], i[1][...], False, tb).astype(dtype)

    return _mm(body, (m // bm, n // bn), [a, b],
               [pl.BlockSpec((bm, k), lambda i, j: (i, 0)),
                pl.BlockSpec((bn, k), lambda i, j: (j, 0)) if tb else pl.BlockSpec((k, bn), lambda i, j: (0, j))],
               [jax.ShapeDtypeStruct((m, n), dtype)], [pl.BlockSpec((bm, bn), lambda i, j: (i, j))],
               2 * m * n * k, name, **kw)


def _mlp_up(n2, dg, w, lo, bn=512, sub=256, **kw):
    m, k = n2.shape
    n = w.shape[1]
    off = lo // m

    def body(i, o):
        for s in range(0, bn, sub):
            sl = slice(s, s + sub)
            a = _nn(i[0][...], i[1][:, sl])
            a2 = a * a
            th = jnp.tanh(C0 * a * (1.0 + C1 * a2))
            p1 = 0.5 + 0.5 * th
            o[0][:, sl] = (a * p1).astype(BF)
            der = p1 + (a * (0.5 * C0)) * (1.0 - th * th) * (1.0 + (3.0 * C1) * a2)
            o[1][:, sl] = (i[2][:, sl] * der).astype(BF)

    tile = pl.BlockSpec((m, bn), lambda i, j: (i, j))
    return _mm(body, (1, n // bn), [n2, w, dg],
               [pl.BlockSpec((m, k), lambda i, j: (0, 0)), pl.BlockSpec((k, bn), lambda i, j: (0, j)),
                pl.BlockSpec((m, bn), lambda i, j: (off, j))],
               [jax.ShapeDtypeStruct((m, n), BF)] * 2, [tile, tile], 2 * m * n * k, "mlp_up", **kw)


def _wgrad(lhs, rhs, bm, bn, name, **kw):
    rows = min(v.shape[0] for v in lhs + rhs)

    def pieces(vs, width, pick):
        arrays, specs = [], []
        for v in vs:
            for p in range(v.shape[0] // rows):
                arrays.append(v)
                specs.append(pl.BlockSpec((rows, width), functools.partial(lambda p, i, j: (p, pick(i, j)), p)))
        return arrays, specs

    la, ls = pieces(lhs, bm, lambda i, j: i)
    ra, rs = pieces(rhs, bn, lambda i, j: j)
    n = len(la)
    m, w = lhs[0].shape[1], rhs[0].shape[1]

    def body(i, o):
        acc = _dot(i[0][...], i[n][...], True, False)
        for e in range(1, n):
            acc += _dot(i[e][...], i[n + e][...], True, False)
        o[0][...] = acc.astype(BF)

    return _mm(body, (m // bm, w // bn), la + ra, ls + rs, [jax.ShapeDtypeStruct((m, w), BF)],
               [pl.BlockSpec((bm, bn), lambda i, j: (i, j))], 2 * m * w * rows * n, name, **kw)


def solution(mesh):
    tp = mesh.shape["tp"]

    def body(x, mu1, rs1, g1, g2, dy, wqkv, wo, w1, w2):
        hl, hd, d = wo.shape
        t = x.shape[0]
        ct = t // NC
        sh = ct // tp
        me = lax.axis_index("tp")
        wo2 = wo.reshape(hl * hd, d)
        g1f = g1.astype(F32)
        g2f = g2.astype(F32)
        muc, rsc, g1r = mu1[:, None], rs1[:, None], g1f[None, :]

        def rows(v, c):
            return lax.dynamic_slice_in_dim(v, c * ct + me * sh, sh, 0)

        def rscat(v):
            return lax.psum_scatter(v, "tp", scatter_dimension=0, tiled=True)

        def gather(v):
            return lax.all_gather(v, "tp", axis=0, tiled=True)

        def after(v, dep):
            return lax.optimization_barrier((v, dep))[0]

        def ln2(c, red):
            h1 = rows(x, c).astype(F32) + red.astype(F32)
            xc = h1 - jnp.mean(h1, axis=-1, keepdims=True)
            rs2 = lax.rsqrt(jnp.mean(xc * xc, axis=-1, keepdims=True) + EPS)
            xh2 = xc * rs2
            return (xh2 * g2f).astype(BF), xh2, rs2

        def fwd(c, x):
            n1, qkv = _norm_qkv(x, muc, rsc, g1r, wqkv, c * ct, ct)
            qkvs.append(qkv)
            n1s.append(n1)
            os.append(_attn_fwd(c, qkvs, hl, hd))
            return _matmul(os[c], wo2, False, ct, 1024, "attn_out")[0]

        n1s, qkvs, os = [], [], []
        p0 = fwd(0, x)
        r0 = rscat(p0)
        p1 = fwd(1, after(x, p0))
        r1 = rscat(p1)
        n2a, xh2a, rs2a = ln2(0, after(r0, p1))
        dg, n2_0 = _matmul(dy, w2, True, 1024, 512, "dgate", F32, shard=n2a, cid=0, marks=(3, 5))
        gb0, da0 = _mlp_up(n2_0, dg, w1, 0)
        n2b, xh2b, rs2b = ln2(1, after(r1, da0))
        q0, n2_1 = _matmul(da0, w1, True, ct, 512, "mlp_back", shard=n2b, cid=1, marks=(5, 7))
        s0 = rscat(q0)
        gb1, da1 = _mlp_up(after(n2_1, q0), dg, w1, ct)
        q1 = _matmul(da1, w1, True, ct, 512, "mlp_back")[0]
        s1 = rscat(q1)
        dw2 = _wgrad([gb0, after(gb1, q1)], [dy], 1024, 1024, "dw2")[0]

        def dln2(c, red, xh2, rs2):
            v = rows(dy, c).astype(F32) + _ln_bwd(red.astype(F32), xh2, rs2, g2f)
            return v, v.astype(BF)

        dh1a, dha = dln2(0, after(s0, dw2), xh2a, rs2a)
        dh1b, dhb = dln2(1, after(s1, dha), xh2b, rs2b)
        dh1_1 = gather(dhb)
        dh1_0 = gather(after(dha, dhb))
        dw1 = _wgrad([n2_0, n2_1], [da0, after(da1, dhb)], 1024, 1024, "dw1")[0]

        def bwd(c, dh, prev):
            do = _matmul(dh, wo2, True, 512, hl * hd, "dattn_out")[0]
            dqkv, prev = _attn_bwd(c, NC, qkvs, do, prev, hl, hd)
            return dqkv, prev, _matmul(dqkv, wqkv, True, ct, 512, "qkv_back")[0]

        dqkv1, prev, u1 = bwd(1, after(dh1_1, dw1), [])
        v1 = rscat(u1)
        dqkv0, prev, u0 = bwd(0, after(dh1_0, u1), prev)
        v0 = rscat(u0)

        def dln1(c, red, dh1):
            xh1 = (rows(x, c).astype(F32) - rows(muc, c)) * rows(rsc, c)
            return (dh1 + _ln_bwd(red.astype(F32), xh1, rows(rsc, c), g1f)).astype(BF)

        dwqkv = _wgrad(n1s, [after(dqkv0, u0), dqkv1], 1024, dqkv0.shape[1] // 2, "dwqkv")[0]
        dwo = _wgrad(os, [after(dh1_0, u0), dh1_1], hl * hd, 1024, "dwo")[0]
        dxb = dln1(1, after(v1, dwqkv), dh1b)
        dxa = dln1(0, after(v0, dxb), dh1a)
        dx = lax.all_gather(jnp.stack([dxa, dxb], 0), "tp", axis=1, tiled=True).reshape(t, d)
        return dx, dwqkv, dwo.reshape(hl, hd, d), dw1, dw2

    return jax.shard_map(
        body, mesh=mesh,
        in_specs=(P("dp", None), P("dp"), P("dp"), P(None), P(None), P("dp", None),
                  P(None, "tp"), P("tp", None, None), P(None, "tp"), P("tp", None)),
        out_specs=(P("dp", None), P("dp", "tp"), P(("dp", "tp"), None, None), P("dp", "tp"), P(("dp", "tp"), None)),
        check_vma=False)
```

time: 1160 us -> 682 us (0.59)
  Pallas kernels: 0 us -> 511 us
  matrix products: 508 us -> 0 us
  waiting for transfers between devices: 379 us -> 91.4 us
  other arithmetic: 216 us -> 39 us
  local copies, waits for them, and re-layouts: 36.2 us -> 19 us
    pallas_call x0 -> x21, Pallas kernels: none -> 511 us  [the longest x13 282 us: _mm(): pl.pallas_call(plain, grid=grid, in_specs=in_specs, out_specs=out_specs,...]
    dot_general x39 -> x0, matrix products: 508 us -> none  [the longest x1 56.5 us: body(): a = jnp.dot(n2, w1, preferred_element_type=f32)]
    psum x3 -> x0, waiting for transfers between devices: 379 us -> none  [the longest x1 131 us: body(): h1 = xf + lax.psum(attn, 'tp').astype(f32)]
    all_gather x0 -> x3, waiting for transfers between devices: none -> 72.3 us  [the longest x1 68.2 us: body(): lax.all_gather(jnp.stack([dxa, dxb], 0), 'tp', axis=1, tiled=True)]
    convert_element_type x8 -> x7, other arithmetic: 79 us -> 17.7 us  [the longest x2 8.63 us: dln2(): return (v, v.astype(BF))]
    reduce_sum x10 -> x4, other arithmetic: 66.8 us -> 7.48 us  [the longest x2 3.99 us: ln2(): xc = h1 - jnp.mean(h1, axis=-1, keepdims=True)]
    add x1 -> x0, other arithmetic: 33.8 us -> none  [body(): dh1 = dy.astype(f32) + _ln_bwd(dn2, xh2, rs2, g2f)]
    reduce_sum x2 -> x4, other arithmetic: 35.9 us -> 9.77 us  [_ln_bwd(): jnp.mean(u, axis=-1, keepdims=True)]
  transfers between devices with their start and end apart: 3 -> 9, of which waited for: 3 -> 4; matrix products, arithmetic and copies ran while one was open for 13% -> 3% of each run, Pallas kernels for 0% -> 63%
where the time goes in v1:
time: 682 us; the launch traced here: 676 us
  Pallas kernels  511 us (75%)
  waiting for transfers between devices  91.4 us (13%)
  other arithmetic  39 us (6%)
  local copies, waits for them, and re-layouts  19 us (3%)
  between operations  14.2 us (2%)
    pallas_call x13, Pallas kernels, _mm(): pl.pallas_call(plain, grid=grid, in_specs=in_specs, out_specs=out_specs,...  282 us
    pallas_call x2, Pallas kernels, _mm(): pl.pallas_call(comm, grid=grid, in_specs=in_specs + [any_spec], out_specs...  108 us
    all_gather x1, waiting for transfers between devices, body(): lax.all_gather(jnp.stack([dxa, dxb], 0), 'tp', axis=1, tiled=True)  68.2 us
    pallas_call x2, Pallas kernels, _attn_bwd(): pl.pallas_call(functools.partial(_attn_bwd_kernel, chunk, nc), grid=(hl,)...  50.1 us
    pallas_call x2, Pallas kernels, _norm_qkv(): pl.pallas_call(_norm_qkv_kernel, grid=(rows // bm,), in_specs=[pl.BlockSp...  40.9 us
    pallas_call x2, Pallas kernels, _attn_fwd(): pl.pallas_call(functools.partial(_attn_fwd_kernel, chunk), grid=(hl,), in...  29.4 us
    reduce_scatter x6, waiting for transfers between devices, rscat(): return lax.psum_scatter(v, 'tp', scatter_dimension=0, tiled=True)  18.1 us
    unnamed x19, local copies, waits for them, and re-layouts  14.1 us
  transfers between devices with their start and end apart: 9, of which 4 were waited for; matrix products, arithmetic and copies ran while one was open for 3% of the time, Pallas kernels for 63%

profile of v1, /device:TPU:113, one launch (start us, length us, event | category | flops | bytes accessed | tf_op | source)
XLA Modules:
  0.0 676.0 jit_solution(10080162937773313456)
XLA Ops:
  7.2 1.3 convert_element_type.58
  8.5 2.0 copy.16.rs_ref
  10.6 2.0 copy.15.mu_ref
  12.6 20.5 %norm_qkv.2 = (bf16[1024,4096]{1,0:T(8,128)(2,1)}, bf16[1024,1536]{1,0:T(8,128)(2,1)}) custom-call(bf16[2048,4096]{1,0:T(8,128)(2,1)} %x_ref.2, f32[2048,1]{1,0:T(8,128)} %copy.15.mu_ref, f32[2048,1]{1,0:T(8,128)} %copy.16.rs_ref, f32[1,4096]{1,0:T(1,128)} %bitcast.11, bf16[4096,1536]{1,0:T(8,128)(2,1)} %refs_1_.13), custom_call_target="tpu_custom_call" | custom-call | flops 12884901888 | bytes 32505856 | tf_op jit(solution)/shard_map/norm_qkv/pallas_call | solution.py:170
  33.1 10.1 %attn_fwd_0.1.refs_0_ = bf16[1024,512]{1,0:T(8,128)(2,1)} custom-call(bf16[1024,1536]{1,0:T(8,128)(2,1)} %get-tuple-element.35.refs_0_), custom_call_target="tpu_custom_call" | custom-call | flops 2147483648 | bytes 4194304 | tf_op jit(solution)/shard_map/attn_fwd_0/pallas_call | solution.py:62
  43.2 8.7 %attn_out.2 = bf16[1024,4096]{1,0:T(8,128)(2,1)} custom-call(bf16[1024,512]{1,0:T(8,128)(2,1)} %attn_fwd_0.1.refs_0_, bf16[512,4096]{1,0:T(8,128)(2,1)} %bitcast.15), custom_call_target="tpu_custom_call" | custom-call | flops 4294967296 | bytes 13631488 | tf_op jit(solution)/shard_map/attn_out/pallas_call | solution.py:278
  52.0 0.4 reduce-scatter.9.cloned.1.call-start
  52.4 20.4 %norm_qkv.3 = (bf16[1024,4096]{1,0:T(8,128)(2,1)}, bf16[1024,1536]{1,0:T(8,128)(2,1)}) custom-call(bf16[2048,4096]{1,0:T(8,128)(2,1)} %x_ref.2, f32[2048,1]{1,0:T(8,128)} %copy.15.mu_ref, f32[2048,1]{1,0:T(8,128)} %copy.16.rs_ref, f32[1,4096]{1,0:T(1,128)} %bitcast.12, bf16[4096,1536]{1,0:T(8,128)(2,1)} %refs_1_.13), custom_call_target="tpu_custom_call" | custom-call | flops 12884901888 | bytes 32505856 | tf_op jit(solution)/shard_map/norm_qkv/pallas_call | solution.py:170
  72.8 19.2 %attn_fwd_1.1.refs_0_.refs_1_ = bf16[1024,512]{1,0:T(8,128)(2,1)} custom-call(bf16[1024,1536]{1,0:T(8,128)(2,1)} %get-tuple-element.35.refs_0_, bf16[1024,1536]{1,0:T(8,128)(2,1)} %get-tuple-element.37.refs_1_), custom_call_target="tpu_custom_call" | custom-call | flops 6442450944 | bytes 8388608 | tf_op jit(solution)/shard_map/attn_fwd_1/pallas_call | solution.py:62
  92.0 8.7 %attn_out.3 = bf16[1024,4096]{1,0:T(8,128)(2,1)} custom-call(bf16[1024,512]{1,0:T(8,128)(2,1)} %attn_fwd_1.1.refs_0_.refs_1_, bf16[512,4096]{1,0:T(8,128)(2,1)} %bitcast.16), custom_call_target="tpu_custom_call" | custom-call | flops 4294967296 | bytes 13631488 | tf_op jit(solution)/shard_map/attn_out/pallas_call | solution.py:278
  100.8 0.6 reduce-scatter.11.cloned.1.call-start
  101.5 1.6 reduce-scatter.7.cloned.1.call-done
  103.1 2.0 fusion.21
  105.1 1.8 multiply_reduce_fusion.3
  106.8 2.7 multiply_convert_fusion.1.refs_2_
  109.5 64.1 %dgate.1 = (f32[2048,2048]{1,0:T(8,128)}, bf16[1024,4096]{1,0:T(8,128)(2,1)}) custom-call(bf16[2048,4096]{1,0:T(8,128)(2,1)} %refs_3_.1, bf16[2048,4096]{1,0:T(8,128)(2,1)} %refs_1_.7, bf16[128,4096]{1,0:T(8,128)(2,1)} %multiply_convert_fusion.1.refs_2_), custom_call_target="tpu_custom_call" | custom-call | flops 34359738368 | bytes 50331648 | tf_op jit(solution)/shard_map/dgate/pallas_call | solution.py:282
  173.6 28.8 %mlp_up.2 = (bf16[1024,2048]{1,0:T(8,128)(2,1)}, bf16[1024,2048]{1,0:T(8,128)(2,1)}) custom-call(bf16[1024,4096]{1,0:T(8,128)(2,1)} %get-tuple-element.39.refs_0_, bf16[4096,2048]{1,0:T(8,128)(2,1)} %refs_1_.11, f32[2048,2048]{1,0:T(8,128)} %get-tuple-element.40.refs_2_), custom_call_target="tpu_custom_call" | custom-call | flops 17179869184 | bytes 50331648 | tf_op jit(solution)/shard_map/mlp_up/pallas_call | solution.py:278
  202.5 2.0 fusion.23
  204.5 1.7 multiply_reduce_fusion.2
  206.2 2.7 multiply_convert_fusion.refs_2_
  208.9 44.2 %mlp_back.2 = (bf16[1024,4096]{1,0:T(8,128)(2,1)}, bf16[1024,4096]{1,0:T(8,128)(2,1)}) custom-call(bf16[1024,2048]{1,0:T(8,128)(2,1)} %get-tuple-element.41.refs_0_.refs_2_, bf16[4096,2048]{1,0:T(8,128)(2,1)} %refs_1_.11, bf16[128,4096]{1,0:T(8,128)(2,1)} %multiply_convert_fusion.refs_2_), custom_call_target="tpu_custom_call" | custom-call | flops 17179869184 | bytes 29360128 | tf_op jit(solution)/shard_map/mlp_back/pallas_call | solution.py:282
  253.5 28.8 %mlp_up.3 = (bf16[1024,2048]{1,0:T(8,128)(2,1)}, bf16[1024,2048]{1,0:T(8,128)(2,1)}) custom-call(bf16[1024,4096]{1,0:T(8,128)(2,1)} %get-tuple-element.46.refs_0_.refs_1_, bf16[4096,2048]{1,0:T(8,128)(2,1)} %refs_1_.11, f32[2048,2048]{1,0:T(8,128)} %get-tuple-element.40.refs_2_), custom_call_target="tpu_custom_call" | custom-call | flops 17179869184 | bytes 50331648 | tf_op jit(solution)/shard_map/mlp_up/pallas_call | solution.py:278
  282.3 22.8 %mlp_back.3 = bf16[1024,4096]{1,0:T(8,128)(2,1)} custom-call(bf16[1024,2048]{1,0:T(8,128)(2,1)} %get-tuple-element.53.refs_0_.refs_3_, bf16[4096,2048]{1,0:T(8,128)(2,1)} %refs_1_.11), custom_call_target="tpu_custom_call" | custom-call | flops 17179869184 | bytes 29360128 | tf_op jit(solution)/shard_map/mlp_back/pallas_call | solution.py:278
  305.2 41.4 %dw2.1 = bf16[2048,4096]{1,0:T(8,128)(2,1)} custom-call(bf16[1024,2048]{1,0:T(8,128)(2,1)} %get-tuple-element.44.refs_0_, bf16[1024,2048]{1,0:T(8,128)(2,1)} %get-tuple-element.49.refs_1_, bf16[2048,4096]{1,0:T(8,128)(2,1)} %refs_3_.1, bf16[2048,4096]{1,0:T(8,128)(2,1)} %refs_3_.1), custom_call_target="tpu_custom_call" | custom-call | flops 34359738368 | bytes 58720256 | tf_op jit(solution)/shard_map/dw2/pallas_call | solution.py:278
  346.6 2.8 fusion.19
  349.5 4.3 fusion.28
  353.8 2.4 fusion.18
  356.3 4.3 fusion.27
  360.7 0.6 all-gather.4.cloned.1.call-update
  361.6 41.4 %dw1.1 = bf16[4096,2048]{1,0:T(8,128)(2,1)} custom-call(bf16[1024,4096]{1,0:T(8,128)(2,1)} %get-tuple-element.39.refs_0_, bf16[1024,4096]{1,0:T(8,128)(2,1)} %get-tuple-element.46.refs_0_.refs_1_, bf16[1024,2048]{1,0:T(8,128)(2,1)} %get-tuple-element.41.refs_0_.refs_2_, bf16[1024,2048]{1,0:T(8,128)(2,1)} %get-tuple-element.53.refs_0_.refs_3_), custom_call_target="tpu_custom_call" | custom-call | flops 34359738368 | bytes 41943040 | tf_op jit(solution)/shard_map/dw1/pallas_call | solution.py:278
  403.0 4.1 all-gather.6.cloned.1.call-done.refs_0_.refs_3_
  407.1 9.0 %dattn_out.2.refs_2_ = bf16[1024,512]{1,0:T(8,128)(2,1)} custom-call(bf16[1024,4096]{1,0:T(8,128)(2,1)} %all-gather.6.cloned.1.call-done.refs_0_.refs_3_, bf16[512,4096]{1,0:T(8,128)(2,1)} %bitcast.17), custom_call_target="tpu_custom_call" | custom-call | flops 4294967296 | bytes 13631488 | tf_op jit(solution)/shard_map/dattn_out/pallas_call | solution.py:278
  416.1 34.2 %attn_bwd_1.1 = (bf16[1024,1536]{1,0:T(8,128)(2,1)}, f32[1024,512]{1,0:T(8,128)}, f32[1024,512]{1,0:T(8,128)}) custom-call(bf16[1024,1536]{1,0:T(8,128)(2,1)} %get-tuple-element.35.refs_0_, bf16[1024,1536]{1,0:T(8,128)(2,1)} %get-tuple-element.37.refs_1_, bf16[1024,512]{1,0:T(8,128)(2,1)} %dattn_out.2.refs_2_), custom_call_target="tpu_custom_call" | custom-call | flops 16106127360 | bytes 12582912 | tf_op jit(solution)/shard_map/attn_bwd_1/pallas_call | solution.py:135
  450.3 18.5 %qkv_back.2 = bf16[1024,4096]{1,0:T(8,128)(2,1)} custom-call(bf16[1024,1536]{1,0:T(8,128)(2,1)} %get-tuple-element.55.refs_0_.refs_3_, bf16[4096,1536]{1,0:T(8,128)(2,1)} %refs_1_.13), custom_call_target="tpu_custom_call" | custom-call | flops 12884901888 | bytes 24117248 | tf_op jit(solution)/shard_map/qkv_back/pallas_call | solution.py:278
  469.0 9.0 %dattn_out.3.refs_1_ = bf16[1024,512]{1,0:T(8,128)(2,1)} custom-call(bf16[1024,4096]{1,0:T(8,128)(2,1)} %all-gather.4.cloned.1.call-done.refs_0_.refs_2_, bf16[512,4096]{1,0:T(8,128)(2,1)} %bitcast.18), custom_call_target="tpu_custom_call" | custom-call | flops 4294967296 | bytes 13631488 | tf_op jit(solution)/shard_map/dattn_out/pallas_call | solution.py:278
  478.0 15.9 %attn_bwd_0.1.refs_0_.refs_2_ = bf16[1024,1536]{1,0:T(8,128)(2,1)} custom-call(bf16[1024,1536]{1,0:T(8,128)(2,1)} %get-tuple-element.35.refs_0_, bf16[1024,512]{1,0:T(8,128)(2,1)} %dattn_out.3.refs_1_, f32[1024,512]{1,0:T(8,128)} %get-tuple-element.57.refs_2_, f32[1024,512]{1,0:T(8,128)} %get-tuple-element.58.refs_3_), custom_call_target="tpu_custom_call" | custom-call | flops 5368709120 | bytes 8388608 | tf_op jit(solution)/shard_map/attn_bwd_0/pallas_call | solution.py:135
  493.9 18.1 %qkv_back.3 = bf16[1024,4096]{1,0:T(8,128)(2,1)} custom-call(bf16[1024,1536]{1,0:T(8,128)(2,1)} %attn_bwd_0.1.refs_0_.refs_2_, bf16[4096,1536]{1,0:T(8,128)(2,1)} %refs_1_.13), custom_call_target="tpu_custom_call" | custom-call | flops 12884901888 | bytes 24117248 | tf_op jit(solution)/shard_map/qkv_back/pallas_call | solution.py:278
  512.1 0.8 fusion.29
  513.0 32.9 %dwqkv.1 = bf16[4096,1536]{1,0:T(8,128)(2,1)} custom-call(bf16[1024,4096]{1,0:T(8,128)(2,1)} %get-tuple-element.59.refs_0_, bf16[1024,4096]{1,0:T(8,128)(2,1)} %get-tuple-element.60.refs_1_, bf16[1024,1536]{1,0:T(8,128)(2,1)} %attn_bwd_0.1.refs_0_.refs_2_, bf16[1024,1536]{1,0:T(8,128)(2,1)} %get-tuple-element.55.refs_0_.refs_3_), custom_call_target="tpu_custom_call" | custom-call | flops 25769803776 | bytes 35651584 | tf_op jit(solution)/shard_map/dwqkv/pallas_call | solution.py:278
  545.9 2.4 fusion.17
  548.3 2.4 fusion.15
  550.8 16.5 %reduce-scatter.15.cloned.1.call-done = bf16[128,4096]{1,0:T(8,128)(2,1)} async-done(((bf16[1024,4096]{1,0:T(8,128)(2,1)}), bf16[128,4096]{1,0:T(8,128)(2,1)}) %reduce-scatter.15.cloned.1.call-update) | async-done | bytes 1048592 | tf_op jit(solution)/shard_map/reduce_scatter | solution.py:370
  567.2 2.2 fusion.16
  569.5 2.4 fusion.26
  571.9 1.5 pad_maximum_fusion
  573.5 13.6 %dwo.1 = bf16[512,4096]{1,0:T(8,128)(2,1)} custom-call(bf16[1024,512]{1,0:T(8,128)(2,1)} %attn_fwd_0.1.refs_0_, bf16[1024,512]{1,0:T(8,128)(2,1)} %attn_fwd_1.1.refs_0_.refs_1_, bf16[1024,4096]{1,0:T(8,128)(2,1)} %all-gather.4.cloned.1.call-done.refs_0_.refs_2_, bf16[1024,4096]{1,0:T(8,128)(2,1)} %all-gather.6.cloned.1.call-done.refs_0_.refs_3_), custom_call_target="tpu_custom_call" | custom-call | flops 8589934592 | bytes 23068672 | tf_op jit(solution)/shard_map/dwo/pallas_call | solution.py:278
  587.1 68.2 %all-gather.8.cloned.1.call-done = bf16[2,1024,4096]{2,1,0:T(8,128)(2,1)} async-done(((bf16[2,128,4096]{2,1,0:T(8,128)(2,1)}), bf16[2,1024,4096]{2,1,0:T(8,128)(2,1)}) %all-gather.8.cloned.1.call-update) | async-done | bytes 16777232 | tf_op jit(solution)/shard_map/all_gather | solution.py:436
  655.2 14.1 %copy.20 = bf16[2048,4096]{1,0:T(8,128)(2,1)} copy(bf16[2048,4096]{1,0:T(8,128)(2,1)} %bitcast.9) | data formatting | bytes 33554432
  (50 shorter events, 1.4 us)
Async XLA Ops:
  7.2 95.9 %reduce-scatter.7.cloned.1.call-start = ((), (), s32[]{:S(2)}) async-start(), calls=%async_computation.6 | async-start | bytes 9437184 | tf_op jit(solution)/shard_map/reduce_scatter | solution.py:370
  52.0 150.5 %reduce-scatter.9.cloned.1.call-start = ((), (), s32[]{:S(2)}) async-start(), calls=%async_computation.7 | async-start | bytes 9437184 | tf_op jit(solution)/shard_map/reduce_scatter | solution.py:370
  100.8 0.7 copy-start.8
  100.8 245.8 %reduce-scatter.11.cloned.1.call-start = ((), (), s32[]{:S(2)}) async-start(), calls=%async_computation.8 | async-start | bytes 9437184 | tf_op jit(solution)/shard_map/reduce_scatter | solution.py:370
  103.1 2.0 copy-start.1
  202.5 2.0 copy-start
  253.2 100.6 %reduce-scatter.13.cloned.1.call-start = ((), (), s32[]{:S(2)}) async-start(), calls=%async_computation.9 | async-start | bytes 9437184 | tf_op jit(solution)/shard_map/reduce_scatter | solution.py:370
  305.2 102.0 %all-gather.6.cloned.1.call-start = ((), (), s32[]{:S(2)}) async-start(), calls=%async_computation.11 | async-start | bytes 9437184 | tf_op jit(solution)/shard_map/all_gather | solution.py:373
  346.6 2.8 copy-start.2
  346.6 2.8 copy-start.6
  353.8 2.4 copy-start.5
  360.6 108.3 %all-gather.4.cloned.1.call-start = ((), (), s32[]{:S(2)}) async-start(), calls=%async_computation.10 | async-start | bytes 9437184 | tf_op jit(solution)/shard_map/all_gather | solution.py:373
  361.3 184.6 %reduce-scatter.17.cloned.1.call-start = ((), (), s32[]{:S(2)}) async-start(), calls=%async_computation.13 | async-start | bytes 9437184 | tf_op jit(solution)/shard_map/reduce_scatter | solution.py:370
  468.9 98.4 %reduce-scatter.15.cloned.1.call-start = ((), (), s32[]{:S(2)}) async-start(), calls=%async_computation.12 | async-start | bytes 9437184 | tf_op jit(solution)/shard_map/reduce_scatter | solution.py:370
  512.1 143.2 %all-gather.8.cloned.1.call-start = ((), (), s32[]{:S(2)}) async-start(), calls=%async_computation.14 | async-start | bytes 18874368 | tf_op jit(solution)/shard_map/all_gather | solution.py:436
  513.0 33.0 %copy-start.7 = (f32[4096]{0:T(1024)S(1)}, f32[4096]{0:T(1024)}, u32[]{:S(2)}) copy-start(f32[4096]{0:T(1024)} %convert_element_type.58) | copy-start | bytes 49156
  545.9 2.4 copy-start.4
  550.7 18.7 %copy-start.3 = (f32[128,4096]{1,0:T(8,128)S(1)}, f32[128,4096]{1,0:T(8,128)}, u32[]{:S(2)}) copy-start(f32[128,4096]{1,0:T(8,128)} %get-tuple-element.76) | copy-start | bytes 6291460
Sparse Core Ops, SparseCore 0:
  52.1 50.8 reduce-scatter.6
  105.9 81.7 reduce-scatter.8
  253.4 48.4 reduce-scatter.10
  305.3 48.4 reduce-scatter.12
  360.8 46.3 all-gather.5
  408.6 45.6 all-gather.3
  469.0 47.7 reduce-scatter.16
  519.1 48.0 reduce-scatter.14
  573.6 81.5 all-gather.7

commit v2 on v1

v2 whole, which is shorter than its diff:
```python
import functools

import jax
import jax.numpy as jnp
from jax import lax
from jax.experimental import pallas as pl
from jax.experimental.pallas import tpu as pltpu
from jax.sharding import PartitionSpec as P

EPS = 1.0 / 100000
F32 = jnp.float32
BF = jnp.bfloat16
NC = 2
BQ = 256
ROWS = 32
LOG2E = 1.4426950408889634


def _mean(x):
    return jnp.mean(x, axis=-1, keepdims=True)


def _ln_bwd(dn, xh, rs, g):
    u = dn * g
    return rs * (u - _mean(u) - xh * _mean(u * xh))


def _nt(a, b):
    return lax.dot_general(a, b, (((1,), (1,)), ((), ())), preferred_element_type=F32)


def _tn(a, b):
    return lax.dot_general(a, b, (((0,), (0,)), ((), ())), preferred_element_type=F32)


def _nn(a, b):
    return jnp.dot(a, b, preferred_element_type=F32)


def _max(x, axis):
    return jnp.max(x, axis=axis, keepdims=True)


def _sum(x, axis):
    return jnp.sum(x, axis=axis, keepdims=True)


def _total(xs):
    return functools.reduce(jnp.add, xs)


def _columns(hd):
    return [slice(e * hd, (e + 1) * hd) for e in range(3)]


def _parts(chunk, rows, b, bq):
    lo = b * bq
    parts = [(c, slice(0, rows)) for c in range(chunk)]
    if b:
        parts.append((chunk, slice(0, lo)))
    return parts + [(chunk, slice(lo, lo + bq))]


def _attn_fwd_kernel(chunk, *refs):
    qkv, o_ref = refs[:-1], refs[-1]
    rows, hd = o_ref.shape
    qc, kc, vc = _columns(hd)
    scale = hd ** -0.5 * LOG2E
    bq = min(BQ, rows)
    mask = lax.broadcasted_iota(jnp.int32, (bq, bq), 0) >= lax.broadcasted_iota(jnp.int32, (bq, bq), 1)
    for b in range(rows // bq):
        parts = _parts(chunk, rows, b, bq)
        me = parts[-1][1]
        q = qkv[chunk][me, qc]
        s = [_nt(q, qkv[c][sl, kc]) for c, sl in parts]
        s[-1] = jnp.where(mask, s[-1], -jnp.inf)
        m = functools.reduce(jnp.maximum, [_max(x, -1) for x in s]) * scale
        p = [jnp.exp2(x * scale - m) for x in s]
        inv = 1.0 / _total([_sum(x, -1) for x in p])
        o = _total([_nn(x.astype(BF), qkv[c][sl, vc]) for x, (c, sl) in zip(p, parts)])
        o_ref[me, :] = (o * inv).astype(BF)


def _attn_fwd(chunk, qkvs, hl, hd):
    rows = qkvs[0].shape[0]
    pairs = rows * rows * chunk + rows * rows // 2
    return pl.pallas_call(
        functools.partial(_attn_fwd_kernel, chunk),
        grid=(hl,),
        in_specs=[pl.BlockSpec((rows, 3 * hd), lambda h: (0, h)) for _ in range(chunk + 1)],
        out_specs=pl.BlockSpec((rows, hd), lambda h: (0, h)),
        out_shape=jax.ShapeDtypeStruct((rows, hl * hd), BF),
        compiler_params=pltpu.CompilerParams(vmem_limit_bytes=60 * 2 ** 20),
        cost_estimate=pl.CostEstimate(flops=8 * hl * pairs * hd, bytes_accessed=rows * hl * hd * 8 * (chunk + 1), transcendentals=hl * pairs),
        name=f"attn_fwd_{chunk}",
    )(*qkvs[:chunk + 1])


def _attn_bwd_kernel(chunk, late, *refs):
    qkv, do_ref, refs = refs[:chunk + 1], refs[chunk + 1], list(refs[chunk + 2:])
    prev = (refs.pop(0), refs.pop(0)) if late else ()
    out_ref = refs.pop(0)
    sums = [(refs.pop(0), refs.pop(0)) for _ in range(chunk + 1)]
    rows, hd = do_ref.shape
    qc, kc, vc = _columns(hd)
    scale = hd ** -0.5
    bq = min(BQ, rows)
    mask = lax.broadcasted_iota(jnp.int32, (bq, bq), 1) >= lax.broadcasted_iota(jnp.int32, (bq, bq), 0)
    for b in range(rows // bq):
        parts = _parts(chunk, rows, b, bq)
        me = parts[-1][1]
        q = qkv[chunk][me, qc]
        do = do_ref[me, :]
        s = [_nt(qkv[c][sl, kc], q) for c, sl in parts]
        s[-1] = jnp.where(mask, s[-1], -jnp.inf)
        m = functools.reduce(jnp.maximum, [_max(x, 0) for x in s]) * (scale * LOG2E)
        p = [jnp.exp2(x * (scale * LOG2E) - m) for x in s]
        inv = 1.0 / _total([_sum(x, 0) for x in p])
        p = [x * inv for x in p]
        dp = [_nt(qkv[c][sl, vc], do) for c, sl in parts]
        r = _total([_sum(x * y, 0) for x, y in zip(p, dp)])
        dq = []
        for x, y, (c, sl) in zip(p, dp, parts):
            ds = (x * (y - r)).astype(BF)
            new = (_nn(ds, q), _nn(x.astype(BF), do))
            dq.append(_tn(ds, qkv[c][sl, kc]))
            fresh = sl is me if c == chunk else b == 0
            for e, (acc, v) in enumerate(zip(sums[c], new)):
                if not fresh:
                    v += acc[sl, :]
                elif c == chunk and late:
                    v += prev[e][sl, :]
                acc[sl, :] = v
        out_ref[me, qc] = (_total(dq) * scale).astype(BF)
    acc_k, acc_v = sums[chunk]
    out_ref[:, kc] = (acc_k[...] * scale).astype(BF)
    out_ref[:, vc] = acc_v[...].astype(BF)


def _attn_bwd(chunk, nc, qkvs, do, prev, hl, hd):
    rows = do.shape[0]
    pairs = rows * rows * chunk + rows * rows // 2
    wide = pl.BlockSpec((rows, 3 * hd), lambda h: (0, h))
    one = pl.BlockSpec((rows, hd), lambda h: (0, h))
    res = pl.pallas_call(
        functools.partial(_attn_bwd_kernel, chunk, chunk < nc - 1),
        grid=(hl,),
        in_specs=[wide] * (chunk + 1) + [one] + [one] * len(prev),
        out_specs=[wide] + [one] * (2 * chunk),
        out_shape=[jax.ShapeDtypeStruct((rows, 3 * hl * hd), BF)]
        + [jax.ShapeDtypeStruct((rows, hl * hd), F32)] * (2 * chunk),
        scratch_shapes=[pltpu.VMEM((rows, hd), F32), pltpu.VMEM((rows, hd), F32)],
        compiler_params=pltpu.CompilerParams(vmem_limit_bytes=62 * 2 ** 20),
        cost_estimate=pl.CostEstimate(flops=20 * hl * pairs * hd, bytes_accessed=rows * hl * hd * 8 * (chunk + 2), transcendentals=hl * pairs),
        name=f"attn_bwd_{chunk}",
    )(*qkvs[:chunk + 1], do, *prev)
    return res[0], list(res[1:])


MESH = pl.DeviceIdType.MESH
VMEM = 62 * 2 ** 20
C0 = 0.7978845608028654
C1 = 0.044715


def _dot(a, b, ta, tb):
    return lax.dot_general(a, b, (((0 if ta else 1,), (1 if tb else 0,)), ((), ())), preferred_element_type=F32)


def _column(v):
    return jnp.transpose(jnp.broadcast_to(v, (128, v.shape[1])))[:, :1]


def _norm_qkv_kernel(x_ref, mu_ref, rs_ref, g_ref, w_ref, n_ref, o_ref):
    xh = (x_ref[...].astype(F32) - _column(mu_ref[...])) * _column(rs_ref[...])
    n_ref[...] = (xh * g_ref[...]).astype(BF)
    o_ref[...] = _nn(n_ref[...], w_ref[...]).astype(BF)


def _norm_qkv(x, mu, rs, g, w, lo, rows):
    bm = 256
    d, n = w.shape
    off = lo // bm
    return pl.pallas_call(
        _norm_qkv_kernel,
        grid=(rows // bm,),
        in_specs=[pl.BlockSpec((bm, d), lambda i: (i + off, 0)),
                  pl.BlockSpec((1, bm), lambda i: (0, i + off)),
                  pl.BlockSpec((1, bm), lambda i: (0, i + off)),
                  pl.BlockSpec((1, d), lambda i: (0, 0)),
                  pl.BlockSpec((d, n), lambda i: (0, 0))],
        out_specs=[pl.BlockSpec((bm, d), lambda i: (i, 0)), pl.BlockSpec((bm, n), lambda i: (i, 0))],
        out_shape=[jax.ShapeDtypeStruct((rows, d), BF), jax.ShapeDtypeStruct((rows, n), BF)],
        compiler_params=pltpu.CompilerParams(vmem_limit_bytes=VMEM),
        cost_estimate=pl.CostEstimate(flops=2 * rows * d * n, bytes_accessed=2 * (2 * rows * d + d * n + rows * n), transcendentals=0),
        name="norm_qkv",
    )(x, mu, rs, g, w)


def _gather_plan(shard, out, local, ssem, rsem):
    tp = lax.axis_size("tp")
    me = lax.axis_index("tp")
    chips = tp // 2
    chip, core = me // 2, lax.rem(me, 2)
    sr = shard.shape[0]
    h = sr // 2

    def dev(shift, other=0):
        k = 1 - core if other else core
        return lax.rem(chip + shift, chips) * 2 + k

    right, left, opp, mate = dev(1), dev(chips - 1), dev(2), dev(0, 1)

    def rows(owner, part=None):
        if part is None:
            return out.at[pl.ds(pl.multiple_of(owner * sr, 8), sr)]
        return out.at[pl.ds(pl.multiple_of(owner * sr + part * h, 8), h)]

    def copy(i, src, dst, to):
        return pltpu.make_async_remote_copy(src_ref=src, dst_ref=dst, send_sem=ssem.at[i], recv_sem=rsem.at[i],
                                            device_id={"tp": to}, device_id_type=MESH)

    lo, hi = shard.at[pl.ds(0, h)], shard.at[pl.ds(h, h)]
    moves = [(lo, rows(me, 0), right), (hi, rows(me, 1), left), (hi, rows(me, 1), right), (lo, rows(me, 0), left), (shard, rows(me), mate)]
    for v, to in ((rows(left, 0), right), (rows(right, 1), left), (rows(left), mate), (rows(right), mate), (rows(opp), mate)):
        moves.append((v, v, to))
    sends = [copy(i, *move) for i, move in enumerate(moves)]
    lands = [rows(left, 0), rows(right, 1), rows(left, 1), rows(right, 0), rows(mate), rows(opp, 0), rows(opp, 1),
             rows(dev(chips - 1, 1)), rows(dev(1, 1)), rows(dev(2, 1))]

    def landed(i):
        copy(i, lands[i], lands[i], mate).wait_recv()

    own = pltpu.make_async_copy(shard, rows(me), local)

    def begin():
        for i in range(5):
            sends[i].start()
        own.start()

    def forward():
        landed(0)
        sends[5].start()
        landed(1)
        sends[6].start()

    def share():
        landed(2)
        sends[7].start()
        landed(3)
        sends[8].start()

    def finish():
        landed(5)
        landed(6)
        sends[9].start()
        for i in (4, 7, 8, 9):
            landed(i)
        own.wait()
        for cp in sends:
            cp.wait_send()

    return (left, right, mate), begin, forward, share, finish


def _gather_events(step, marks, *refs):
    peers, begin, forward, share, finish = _gather_plan(*refs)

    @pl.when(step == 0)
    def _():
        bar = pltpu.get_barrier_semaphore()
        for to in peers:
            pl.semaphore_signal(bar, inc=1, device_id={"tp": to}, device_id_type=MESH)
        pl.semaphore_wait(bar, 3)
        begin()

    pl.when(step == marks[0])(forward)
    pl.when(step == marks[1])(share)
    return finish


def _gather_all(*refs):
    for stage in _gather_plan(*refs)[1:]:
        stage()


def _mm(body, grid, ins, in_specs, outs, out_specs, flops, name, shard=None, cid=0, marks=(0, 0)):
    n_in, n_out = len(ins), len(outs)
    steps = grid[0] * grid[1]

    def plain(*refs):
        body(refs[:n_in], refs[n_in:])

    def comm(*refs):
        sh, out = refs[n_in], refs[n_in + 1 + n_out]
        step = pl.program_id(0) * grid[1] + pl.program_id(1)
        finish = _gather_events(step, marks, sh, out, *refs[n_in + n_out + 2:])
        body(refs[:n_in], refs[n_in + 1:n_in + 1 + n_out])
        pl.when(step == steps - 1)(finish)

    nbytes = sum(v.size * v.dtype.itemsize for v in ins) + sum(v.size * v.dtype.itemsize for v in outs)
    cost = pl.CostEstimate(flops=flops, bytes_accessed=nbytes, transcendentals=0)
    if shard is None:
        res = pl.pallas_call(plain, grid=grid, in_specs=in_specs, out_specs=out_specs, out_shape=outs, cost_estimate=cost,
                              compiler_params=pltpu.CompilerParams(vmem_limit_bytes=VMEM), name=name)(*ins)
        return res[0] if n_out == 1 else res
    any_spec = pl.BlockSpec(memory_space=pl.ANY)
    full = jax.ShapeDtypeStruct((shard.shape[0] * lax.axis_size("tp"), shard.shape[1]), shard.dtype)
    return pl.pallas_call(
        comm, grid=grid, in_specs=in_specs + [any_spec], out_specs=out_specs + [any_spec], out_shape=outs + [full],
        scratch_shapes=[pltpu.SemaphoreType.DMA, pltpu.SemaphoreType.DMA((10,)), pltpu.SemaphoreType.DMA((10,))],
        cost_estimate=cost, name=name,
        compiler_params=pltpu.CompilerParams(vmem_limit_bytes=VMEM, collective_id=cid, has_side_effects=True))(*ins, shard)


def _matmul(a, b, tb, bm, bn, name, dtype=BF, **kw):
    m, k = a.shape
    n = b.shape[0] if tb else b.shape[1]

    def body(i, o):
        o[0][...] = _dot(i[0][...], i[1][...], False, tb).astype(dtype)

    return _mm(body, (m // bm, n // bn), [a, b],
               [pl.BlockSpec((bm, k), lambda i, j: (i, 0)),
                pl.BlockSpec((bn, k), lambda i, j: (j, 0)) if tb else pl.BlockSpec((k, bn), lambda i, j: (0, j))],
               [jax.ShapeDtypeStruct((m, n), dtype)], [pl.BlockSpec((bm, bn), lambda i, j: (i, j))],
               2 * m * n * k, name, **kw)


def _mlp_up(n2, dg, w, lo, part=0, parts=1, prev=(), bn=512, sub=256):
    m, k = n2.shape
    n = w.shape[1]
    bm = m // parts
    off = lo // bm + part

    def body(n2_ref, w_ref, dg_ref, *rest):
        gb_ref, da_ref = rest[-2:]

        def finish(s, a):
            sl = slice(s, s + sub)
            a2 = a * a
            th = jnp.tanh(a * (C0 + (C0 * C1) * a2))
            p1 = 0.5 + 0.5 * th
            gb_ref[:, sl] = (a * p1).astype(BF)
            der = p1 + (a - a * (th * th)) * (0.5 * C0 + (1.5 * C0 * C1) * a2)
            da_ref[:, sl] = (dg_ref[:, sl] * der).astype(BF)

        held = None
        for s in range(0, bn, sub):
            a = _nn(n2_ref[...], w_ref[:, s:s + sub])
            if held is not None:
                finish(*held)
            held = (s, a)
        finish(*held)

    tile = pl.BlockSpec((bm, bn), lambda j: (part, j))
    return pl.pallas_call(
        body, grid=(n // bn,),
        in_specs=[pl.BlockSpec((bm, k), lambda j: (part, 0)), pl.BlockSpec((k, bn), lambda j: (0, j)),
                  pl.BlockSpec((bm, bn), lambda j: (off, j))] + [pl.BlockSpec(memory_space=pl.ANY)] * len(prev),
        out_specs=[tile, tile], out_shape=[jax.ShapeDtypeStruct((m, n), BF)] * 2,
        input_output_aliases={3: 0, 4: 1} if prev else {},
        cost_estimate=pl.CostEstimate(flops=2 * bm * n * k, bytes_accessed=2 * (bm * k + k * n) + 8 * bm * n, transcendentals=bm * n),
        compiler_params=pltpu.CompilerParams(vmem_limit_bytes=VMEM), name="mlp_up")(n2, w, dg, *prev)


def _wgrad(lhs, rhs, bm, bn, name, **kw):
    rows = min(v.shape[0] for v in lhs + rhs)

    def pieces(vs, width, pick):
        arrays, specs = [], []
        for v in vs:
            for p in range(v.shape[0] // rows):
                arrays.append(v)
                specs.append(pl.BlockSpec((rows, width), functools.partial(lambda p, i, j: (p, pick(i, j)), p)))
        return arrays, specs

    la, ls = pieces(lhs, bm, lambda i, j: i)
    ra, rs = pieces(rhs, bn, lambda i, j: j)
    n = len(la)
    m, w = lhs[0].shape[1], rhs[0].shape[1]

    def body(i, o):
        acc = _dot(i[0][...], i[n][...], True, False)
        for e in range(1, n):
            acc += _dot(i[e][...], i[n + e][...], True, False)
        o[0][...] = acc.astype(BF)

    return _mm(body, (m // bm, w // bn), la + ra, ls + rs, [jax.ShapeDtypeStruct((m, w), BF)],
               [pl.BlockSpec((bm, bn), lambda i, j: (i, j))], 2 * m * w * rows * n, name, **kw)


def _turn(part, xh, rs, g, skip, other, lhs, rhs, bm, bn, cid):
    tp = lax.axis_size("tp")
    chips = tp // 2
    t, d = part.shape
    sr = t // tp
    h = sr // 2
    n = len(lhs)
    rows = lhs[0].shape[0]
    m, w = lhs[0].shape[1], rhs[0].shape[1]
    grid = (m // bm, w // bn)
    steps = grid[0] * grid[1]
    arrays, specs = [], []
    for vs, width, pick in ((lhs, bm, lambda i, j: i), (rhs, bn, lambda i, j: j)):
        for v in vs:
            for p in range(v.shape[0] // rows):
                arrays.append(v)
                specs.append(pl.BlockSpec((rows, width), functools.partial(lambda pick, p, i, j: (p, pick(i, j)), pick, p)))
    n = len(arrays) // 2

    def kernel(*refs):
        ins, refs = refs[:2 * n], refs[2 * n:]
        part_ref, xh_ref, rs_ref, g_ref, skip_ref, refs = *refs[:5], refs[5:]
        other_in, (dw_ref, dh_ref, dh0_ref, dhb0_ref, full), refs = refs[:4], refs[4:9], refs[9:]
        own, mates, sums, fromleft, fromright, l1, r1, shard, lsem, asem, bsem, csem, dsem, gl, gs, gr = refs
        me = lax.axis_index("tp")
        chip, core = me // 2, lax.rem(me, 2)
        step = pl.program_id(0) * grid[1] + pl.program_id(1)
        order = [lax.rem(chip + e, chips) for e in (2, 1, chips - 1, 0)]
        right, left, mate = order[1] * 2 + core, order[2] * 2 + core, chip * 2 + 1 - core

        def block(c, k):
            return part_ref.at[pl.ds(pl.multiple_of((2 * c + k) * sr, 8), sr)]

        def remote(src, dst, ssem, rsem, to):
            return pltpu.make_async_remote_copy(src_ref=src, dst_ref=dst, send_sem=ssem, recv_sem=rsem,
                                                device_id={"tp": to}, device_id_type=MESH)

        loads = [pltpu.make_async_copy(block(order[e], core), own.at[e], lsem.at[e]) for e in range(4)]
        swaps = [remote(block(order[e], 1 - core), mates.at[e], asem.at[e], bsem.at[e], mate) for e in range(4)]
        lo, hi = pl.ds(0, h), pl.ds(h, h)
        legs = [(sums.at[0, lo], l1, right), (sums.at[0, hi], r1, left),
                (sums.at[1, hi], fromleft.at[hi], right), (sums.at[2, lo], fromright.at[lo], left),
                (sums.at[1, lo], fromleft.at[lo], right), (sums.at[2, hi], fromright.at[hi], left)]
        hops = [remote(src, dst, csem.at[e], dsem.at[e], to) for e, (src, dst, to) in enumerate(legs)]

        def pair(e, sl):
            return own[e, sl].astype(F32) + mates[e, sl].astype(F32)

        def ready(e):
            loads[e].wait()
            swaps[e].wait_recv()

        @pl.when(step == 0)
        def _():
            bar = pltpu.get_barrier_semaphore()
            for to in (left, right, mate):
                pl.semaphore_signal(bar, inc=1, device_id={"tp": to}, device_id_type=MESH)
            pl.semaphore_wait(bar, 3)
            for e in range(4):
                loads[e].start()
                swaps[e].start()

        @pl.when(step == 1)
        def _():
            ready(0)
            sums[0] = pair(0, pl.ds(0, sr)).astype(BF)
            hops[0].start()
            hops[1].start()
            ready(1)
            ready(2)
            sums[1, hi] = pair(1, hi).astype(BF)
            hops[2].start()
            sums[2, lo] = pair(2, lo).astype(BF)
            hops[3].start()

        @pl.when(step == 4)
        def _():
            hops[0].wait_recv()
            sums[1, lo] = (pair(1, lo) + l1[...].astype(F32)).astype(BF)
            hops[4].start()
            hops[1].wait_recv()
            sums[2, hi] = (pair(2, hi) + r1[...].astype(F32)).astype(BF)
            hops[5].start()
            red0, xh0, rs0, skip0 = other_in
            v0 = skip0[...].astype(F32) + _ln_bwd(red0[...].astype(F32), xh0[...], rs0[...], g_ref[...])
            dh0_ref[...] = v0
            dhb0_ref[...] = v0.astype(BF)

        acc = _dot(ins[0][...], ins[n][...], True, False)
        for e in range(1, n):
            acc += _dot(ins[e][...], ins[n + e][...], True, False)
        dw_ref[...] = acc.astype(BF)

        @pl.when(step == steps - 1)
        def _():
            ready(3)
            for e in (2, 3, 4, 5):
                hops[e].wait_recv()
            total = pair(3, pl.ds(0, sr)) + fromleft[...].astype(F32) + fromright[...].astype(F32)
            v = skip_ref[...].astype(F32) + _ln_bwd(total.astype(BF).astype(F32), xh_ref[...], rs_ref[...], g_ref[...])
            dh_ref[...] = v
            shard[...] = v.astype(BF)
            for cp in swaps:
                cp.wait_send()
            for cp in hops:
                cp.wait_send()
            _gather_all(shard, full, gl, gs, gr)

    one = lambda shape: pl.BlockSpec(shape, lambda i, j: (0, 0), pipeline_mode=pl.Buffered(1))
    res = pl.BlockSpec((sr, d), lambda i, j: (0, 0))
    any_spec = pl.BlockSpec(memory_space=pl.ANY)
    blk = pltpu.VMEM((sr, d), BF)
    sem = pltpu.SemaphoreType.DMA
    return pl.pallas_call(
        kernel, grid=grid,
        in_specs=specs + [any_spec, one((sr, d)), one((sr, 1)), one((1, d)), one((sr, d)),
                          one((sr, d)), one((sr, d)), one((sr, 1)), one((sr, d))],
        out_specs=[pl.BlockSpec((bm, bn), lambda i, j: (i, j)), res, res, res, any_spec],
        out_shape=[jax.ShapeDtypeStruct((m, w), BF), jax.ShapeDtypeStruct((sr, d), F32), jax.ShapeDtypeStruct((sr, d), F32),
                   jax.ShapeDtypeStruct((sr, d), BF), jax.ShapeDtypeStruct((t, d), BF)],
        scratch_shapes=[pltpu.VMEM((4, sr, d), BF), pltpu.VMEM((4, sr, d), BF), pltpu.VMEM((3, sr, d), BF), blk, blk,
                        pltpu.VMEM((h, d), BF), pltpu.VMEM((h, d), BF), blk,
                        sem((4,)), sem((4,)), sem((4,)), sem((6,)), sem((6,)), sem, sem((10,)), sem((10,))],
        cost_estimate=pl.CostEstimate(flops=4 * m * w * rows * n, bytes_accessed=64 * 2 ** 20, transcendentals=0),
        compiler_params=pltpu.CompilerParams(vmem_limit_bytes=VMEM, collective_id=cid, has_side_effects=True),
        name="turn")(*arrays, part, xh, rs, g, skip, *other)


def _rowwise(body, ins, outs, name, slot=0, prev=()):
    sr = ins[0].shape[0]
    grid = sr // ROWS

    def spec(v):
        if len(v.shape) > 2:
            return pl.BlockSpec((None, ROWS, v.shape[-1]), lambda i: (slot, i, 0))
        return pl.BlockSpec((ROWS, v.shape[1]), lambda i: (i, 0)) if v.shape[0] == sr else pl.BlockSpec(v.shape, lambda i: (0, 0))

    return pl.pallas_call(body, grid=(grid,), in_specs=[spec(v) for v in ins] + [pl.BlockSpec(memory_space=pl.ANY)] * len(prev),
                          out_specs=[spec(v) for v in outs], out_shape=outs,
                          input_output_aliases={len(ins): 0} if prev else {},
                          compiler_params=pltpu.CompilerParams(vmem_limit_bytes=VMEM), name=name)(*ins, *prev)


def _norm_kernel(red, x, g, n_ref, xh_ref, rs_ref):
    h1 = x[...].astype(F32) + red[...].astype(F32)
    xc = h1 - _mean(h1)
    rs = lax.rsqrt(_mean(xc * xc) + EPS)
    xh_ref[...] = xc * rs
    rs_ref[...] = rs
    n_ref[...] = (xh_ref[...] * g[...]).astype(BF)


def _dx_kernel(red, x, mu, rs, g, dh, *refs):
    xh = (x[...].astype(F32) - mu[...]) * rs[...]
    refs[-1][...] = (dh[...] + _ln_bwd(red[...].astype(F32), xh, rs[...], g[...])).astype(BF)


def _relay_kernel(i, o):
    o[...] = i[...]


def _relay(v):
    spec = pl.BlockSpec((v.shape[0] // 8, v.shape[1]), lambda i: (i, 0))
    return pl.pallas_call(_relay_kernel, grid=(8,), in_specs=[spec], out_specs=spec, out_shape=jax.ShapeDtypeStruct(v.shape, v.dtype),
                          cost_estimate=pl.CostEstimate(flops=v.size * v.shape[1], bytes_accessed=v.size, transcendentals=0),
                          compiler_params=pltpu.CompilerParams(vmem_limit_bytes=VMEM), name="relay")(v)


def solution(mesh):
    tp = mesh.shape["tp"]

    def body(x, mu1, rs1, g1, g2, dy, wqkv, wo, w1, w2):
        hl, hd, d = wo.shape
        t = x.shape[0]
        ct = t // NC
        sh = ct // tp
        me = lax.axis_index("tp")
        wo2 = wo.reshape(hl * hd, d)
        g1f = g1.astype(F32)
        g2f = g2.astype(F32)
        mur, rsr, g1r = mu1[None, :], rs1[None, :], g1f[None, :]

        def rows(v, c):
            return lax.dynamic_slice_in_dim(v, c * ct + me * sh, sh, 0)

        def rscat(v):
            return lax.psum_scatter(v, "tp", scatter_dimension=0, tiled=True)

        def gather(v):
            return lax.all_gather(v, "tp", axis=0, tiled=True)

        def after(v, dep):
            return lax.optimization_barrier((v, dep))[0]

        def ln2(c, red):
            shard = jax.ShapeDtypeStruct(red.shape, F32)
            outs = [jax.ShapeDtypeStruct(red.shape, BF), shard, jax.ShapeDtypeStruct((sh, 1), F32)]
            return _rowwise(_norm_kernel, [red, xrows[c], g2f[None, :]], outs, "norm2")

        def fwd(c, x):
            n1, qkv = _norm_qkv(x, mur, rsr, g1r, wqkv, c * ct, ct)
            qkvs.append(qkv)
            n1s.append(n1)
            os.append(_attn_fwd(c, qkvs, hl, hd))
            return _matmul(os[c], wo2, False, ct, 1024, "attn_out")

        xrows = [rows(x, c) for c in range(NC)]
        n1s, qkvs, os = [], [], []
        p0 = fwd(0, x)
        r0 = rscat(p0)
        p1 = fwd(1, after(x, p0))
        r1 = rscat(p1)
        n2a, xh2a, rs2a = ln2(0, after(r0, p1))
        dg, n2_0 = _matmul(dy, w2, True, 1024, 512, "dgate", F32, shard=n2a, cid=0, marks=(3, 5))
        half = _mlp_up(n2_0, dg, w1, 0, 0, 2)
        n2b, xh2b, rs2b = ln2(1, after(r1, half[0]))
        n2_1 = gather(n2b)
        gb0, da0 = _mlp_up(after(n2_0, n2b), dg, w1, 0, 1, 2, half)
        q0 = _matmul(da0, w1, True, ct, 512, "mlp_back")
        s0 = rscat(q0)
        gb1, da1 = _mlp_up(after(n2_1, q0), dg, w1, ct)
        q1 = _matmul(da1, w1, True, ct, 512, "mlp_back")
        dw2, dh1b, dh1a, dha, dh1_1 = _turn(q1, xh2b, rs2b, g2f[None, :], rows(dy, 1), (s0, xh2a, rs2a, rows(dy, 0)),
                                            [gb0, gb1], [dy], 1024, 1024, 1)
        dh1_0 = gather(dha)

        def bwd(c, dh, prev):
            do = _matmul(dh, wo2, True, 512, hl * hd, "dattn_out")
            dqkv, prev = _attn_bwd(c, NC, qkvs, do, prev, hl, hd)
            return dqkv, prev, _matmul(dqkv, wqkv, True, ct, 1024, "qkv_back")

        dqkv1, prev, u1 = bwd(1, dh1_1, [])
        v1 = rscat(u1)
        dqkv0, prev, u0 = bwd(0, after(dh1_0, u1), prev)
        v0 = rscat(u0)

        def dln1(c, red, dh1, *prev):
            ins = [red, xrows[c], rows(mu1, c)[:, None], rows(rs1, c)[:, None], g1r, dh1]
            return _rowwise(_dx_kernel, ins, [jax.ShapeDtypeStruct((NC, sh, d), BF)], "dx", c, prev)[0]

        dwqkv = _wgrad(n1s, [after(dqkv0, u0), dqkv1], 1024, dqkv0.shape[1] // 2, "dwqkv")
        dxb = dln1(1, after(v1, dwqkv), dh1b)
        dwo = _wgrad([after(os[0], dxb), os[1]], [dh1_0, dh1_1], hl * hd, 1024, "dwo")
        dxa = dln1(0, after(v0, dwo), dh1a, dxb)
        dx = lax.all_gather(dxa, "tp", axis=1, tiled=True).reshape(t, d)
        dw1 = _wgrad([n2_0, n2_1], [da0, after(da1, dxa)], 1024, 1024, "dw1")
        dw2 = _relay(after(dw2, dw1))
        return dx, dwqkv, dwo.reshape(hl, hd, d), dw1, dw2

    return jax.shard_map(
        body, mesh=mesh,
        in_specs=(P("dp", None), P("dp"), P("dp"), P(None), P(None), P("dp", None),
                  P(None, "tp"), P("tp", None, None), P(None, "tp"), P("tp", None)),
        out_specs=(P("dp", None), P("dp", "tp"), P(("dp", "tp"), None, None), P("dp", "tp"), P(("dp", "tp"), None)),
        check_vma=False)
```

time: 682 us -> 650 us (0.953)
  waiting for transfers between devices: 91.4 us -> 33.5 us
  Pallas kernels: 511 us -> 565 us
  other arithmetic: 39 us -> 1.9 us
    pallas_call x2 -> x11, Pallas kernels: 50.1 us -> 230 us  [the longest x1 91.9 us: _turn(): pl.pallas_call(kernel, grid=grid, in_specs=specs + [any_spec, one((sr, d)...]
    pallas_call x13 -> x11, Pallas kernels: 282 us -> 206 us  [_mm(): pl.pallas_call(plain, grid=grid, in_specs=in_specs, out_specs=out_specs,...]
    pallas_call x2 -> x1, Pallas kernels: 108 us -> 64.1 us  [_mm(): pl.pallas_call(comm, grid=grid, in_specs=in_specs + [any_spec], out_specs...]
    all_gather x1, waiting for transfers between devices: 68.2 us -> 26.5 us  [body(): dx = lax.all_gather(dxa, 'tp', axis=1, tiled=True).reshape(t, d)]
    convert_element_type x7 -> x0, other arithmetic: 17.7 us -> none  [the longest x2 8.63 us: dln2(): return (v, v.astype(BF))]
    reduce_sum x8 -> x0, other arithmetic: 17.3 us -> none  [the longest x4 9.77 us: _ln_bwd(): jnp.mean(u, axis=-1, keepdims=True)]
    reduce_scatter x6 -> x5, waiting for transfers between devices: 18.1 us -> 3.14 us  [rscat(): return lax.psum_scatter(v, 'tp', scatter_dimension=0, tiled=True)]
    unnamed x19 -> x3, local copies, waits for them, and re-layouts: 14.1 us -> 14.1 us
  transfers between devices with their start and end apart: 9 -> 8, of which waited for: 4 -> 4; matrix products, arithmetic and copies ran while one was open for 3% -> 2% of each run, Pallas kernels for 63% -> 67%
where the time goes in v2:
time: 650 us; the launch traced here: 641 us
  Pallas kernels  565 us (87%)
  waiting for transfers between devices  33.5 us (5%)
  local copies, waits for them, and re-layouts  24 us (4%)
  between operations  14.7 us (2%)
    pallas_call x11, Pallas kernels, _mm(): pl.pallas_call(plain, grid=grid, in_specs=in_specs, out_specs=out_specs,...  206 us
    pallas_call x1, Pallas kernels, _turn(): pl.pallas_call(kernel, grid=grid, in_specs=specs + [any_spec, one((sr, d)...  91.9 us
    pallas_call x1, Pallas kernels, _mm(): pl.pallas_call(comm, grid=grid, in_specs=in_specs + [any_spec], out_specs...  64.1 us
    pallas_call x3, Pallas kernels, _mlp_up(): pl.pallas_call(body, grid=(n // bn,), in_specs=[pl.BlockSpec((bm, k), lam...  60.5 us
    pallas_call x2, Pallas kernels, _attn_bwd(): pl.pallas_call(functools.partial(_attn_bwd_kernel, chunk, chunk < nc - 1)...  46.1 us
    pallas_call x2, Pallas kernels, _norm_qkv(): pl.pallas_call(_norm_qkv_kernel, grid=(rows // bm,), in_specs=[pl.BlockSp...  41.7 us
    all_gather x1, waiting for transfers between devices, body(): dx = lax.all_gather(dxa, 'tp', axis=1, tiled=True).reshape(t, d)  26.5 us
    pallas_call x2, Pallas kernels, _attn_fwd(): pl.pallas_call(functools.partial(_attn_fwd_kernel, chunk), grid=(hl,), in...  23.6 us
  transfers between devices with their start and end apart: 8, of which 4 were waited for; matrix products, arithmetic and copies ran while one was open for 2% of the time, Pallas kernels for 67%

profile of v2, /device:TPU:113, one launch (start us, length us, event | category | flops | bytes accessed | tf_op | source)
XLA Modules:
  0.0 640.6 jit_solution(10371788293610684628)
XLA Ops:
  7.2 1.3 broadcast_in_dim.40
  8.5 20.8 %norm_qkv.2 = (bf16[1024,4096]{1,0:T(8,128)(2,1)}, bf16[1024,1536]{1,0:T(8,128)(2,1)}) custom-call(bf16[2048,4096]{1,0:T(8,128)(2,1)} %x_ref.2, f32[1,2048]{1,0:T(1,128)} %bitcast.23, f32[1,2048]{1,0:T(1,128)} %bitcast.25, f32[1,4096]{1,0:T(1,128)} %bitcast.16, bf16[4096,1536]{1,0:T(8,128)(2,1)} %refs_1_.9), custom_call_target="tpu_custom_call" | custom-call | flops 12884901888 | bytes 32505856 | tf_op jit(solution)/shard_map/norm_qkv/pallas_call | solution.py:184
  29.4 8.8 %attn_fwd_0.1.refs_0_ = bf16[1024,512]{1,0:T(8,128)(2,1)} custom-call(bf16[1024,1536]{1,0:T(8,128)(2,1)} %get-tuple-element.43.refs_0_), custom_call_target="tpu_custom_call" | custom-call | flops 2147483648 | bytes 4194304 | tf_op jit(solution)/shard_map/attn_fwd_0/pallas_call | solution.py:87
  38.2 8.7 %attn_out.2 = bf16[1024,4096]{1,0:T(8,128)(2,1)} custom-call(bf16[1024,512]{1,0:T(8,128)(2,1)} %attn_fwd_0.1.refs_0_, bf16[512,4096]{1,0:T(8,128)(2,1)} %bitcast.27), custom_call_target="tpu_custom_call" | custom-call | flops 4294967296 | bytes 13631488 | tf_op jit(solution)/shard_map/attn_out/pallas_call | solution.py:304
  47.0 0.1 reduce-scatter.8.cloned.1.call-start
  47.0 20.9 %norm_qkv.3 = (bf16[1024,4096]{1,0:T(8,128)(2,1)}, bf16[1024,1536]{1,0:T(8,128)(2,1)}) custom-call(bf16[2048,4096]{1,0:T(8,128)(2,1)} %x_ref.2, f32[1,2048]{1,0:T(1,128)} %bitcast.24, f32[1,2048]{1,0:T(1,128)} %bitcast.26, f32[1,4096]{1,0:T(1,128)} %bitcast.17, bf16[4096,1536]{1,0:T(8,128)(2,1)} %refs_1_.9), custom_call_target="tpu_custom_call" | custom-call | flops 12884901888 | bytes 32505856 | tf_op jit(solution)/shard_map/norm_qkv/pallas_call | solution.py:184
  67.9 14.8 %attn_fwd_1.1.refs_0_.refs_1_ = bf16[1024,512]{1,0:T(8,128)(2,1)} custom-call(bf16[1024,1536]{1,0:T(8,128)(2,1)} %get-tuple-element.43.refs_0_, bf16[1024,1536]{1,0:T(8,128)(2,1)} %get-tuple-element.45.refs_1_), custom_call_target="tpu_custom_call" | custom-call | flops 6442450944 | bytes 8388608 | tf_op jit(solution)/shard_map/attn_fwd_1/pallas_call | solution.py:87
  82.7 8.7 %attn_out.3 = bf16[1024,4096]{1,0:T(8,128)(2,1)} custom-call(bf16[1024,512]{1,0:T(8,128)(2,1)} %attn_fwd_1.1.refs_0_.refs_1_, bf16[512,4096]{1,0:T(8,128)(2,1)} %bitcast.28), custom_call_target="tpu_custom_call" | custom-call | flops 4294967296 | bytes 13631488 | tf_op jit(solution)/shard_map/attn_out/pallas_call | solution.py:304
  91.5 0.3 all-gather.4.cloned.1.call-start
  91.8 0.6 broadcast_in_dim.41
  92.4 3.1 constant_dynamic-slice_fusion.2
  95.5 2.5 reduce-scatter.6.cloned.1.call-done.red
  98.0 4.5 norm2.2
  102.5 64.1 %dgate.1 = (f32[2048,2048]{1,0:T(8,128)}, bf16[1024,4096]{1,0:T(8,128)(2,1)}) custom-call(bf16[2048,4096]{1,0:T(8,128)(2,1)} %refs_3_.1, bf16[2048,4096]{1,0:T(8,128)(2,1)} %refs_1_.5, bf16[128,4096]{1,0:T(8,128)(2,1)} %get-tuple-element.47.refs_2_), custom_call_target="tpu_custom_call" | custom-call | flops 34359738368 | bytes 50331648 | tf_op jit(solution)/shard_map/dgate/pallas_call | solution.py:309
  166.6 16.1 %mlp_up.3 = (bf16[1024,2048]{1,0:T(8,128)(2,1)}, bf16[1024,2048]{1,0:T(8,128)(2,1)}) custom-call(bf16[1024,4096]{1,0:T(8,128)(2,1)} %get-tuple-element.53.n2_ref.refs_0_, bf16[4096,2048]{1,0:T(8,128)(2,1)} %refs_1_.7, f32[2048,2048]{1,0:T(8,128)} %get-tuple-element.49.dg_ref), custom_call_target="tpu_custom_call" | custom-call | flops 8589934592 | bytes 29360128 | tf_op jit(solution)/shard_map/mlp_up/pallas_call | solution.py:357
  182.7 4.5 norm2.3
  187.3 0.1 reduce-scatter.10.cloned.1.call-start
  187.4 16.1 %mlp_up.4 = (bf16[1024,2048]{1,0:T(8,128)(2,1)}, bf16[1024,2048]{1,0:T(8,128)(2,1)}) custom-call(bf16[1024,4096]{1,0:T(8,128)(2,1)} %get-tuple-element.53.n2_ref.refs_0_, bf16[4096,2048]{1,0:T(8,128)(2,1)} %refs_1_.7, f32[2048,2048]{1,0:T(8,128)} %get-tuple-element.49.dg_ref, ...), custom_call_target="tpu_custom_call", output_to_operand_aliasing={{0}: (3, {}), {1}: (4, {})} | custom-call | flops 8589934592 | bytes 29360128 | tf_op jit(solution)/shard_map/mlp_up/pallas_call | solution.py:357
  203.5 22.8 %mlp_back.2 = bf16[1024,4096]{1,0:T(8,128)(2,1)} custom-call(bf16[1024,2048]{1,0:T(8,128)(2,1)} %get-tuple-element.56.refs_0_.refs_2_, bf16[4096,2048]{1,0:T(8,128)(2,1)} %refs_1_.7), custom_call_target="tpu_custom_call" | custom-call | flops 17179869184 | bytes 29360128 | tf_op jit(solution)/shard_map/mlp_back/pallas_call | solution.py:304
  226.4 0.5 all-gather.6.cloned.1.call-start
  226.8 3.1 constant_dynamic-slice_fusion
  230.0 3.4 all-gather.4.cloned.1.call-done.n2_ref.refs_1_
  233.4 28.3 %mlp_up.5 = (bf16[1024,2048]{1,0:T(8,128)(2,1)}, bf16[1024,2048]{1,0:T(8,128)(2,1)}) custom-call(bf16[1024,4096]{1,0:T(8,128)(2,1)} %all-gather.4.cloned.1.call-done.n2_ref.refs_1_, bf16[4096,2048]{1,0:T(8,128)(2,1)} %refs_1_.7, f32[2048,2048]{1,0:T(8,128)} %get-tuple-element.49.dg_ref), custom_call_target="tpu_custom_call" | custom-call | flops 17179869184 | bytes 41943040 | tf_op jit(solution)/shard_map/mlp_up/pallas_call | solution.py:357
  261.7 22.8 %mlp_back.3.refs_4_ = bf16[1024,4096]{1,0:T(8,128)(2,1)} custom-call(bf16[1024,2048]{1,0:T(8,128)(2,1)} %get-tuple-element.78.refs_0_.refs_3_, bf16[4096,2048]{1,0:T(8,128)(2,1)} %refs_1_.7), custom_call_target="tpu_custom_call" | custom-call | flops 17179869184 | bytes 29360128 | tf_op jit(solution)/shard_map/mlp_back/pallas_call | solution.py:304
  284.5 91.9 %turn.1 = (bf16[2048,4096]{1,0:T(8,128)(2,1)}, f32[128,4096]{1,0:T(8,128)}, f32[128,4096]{1,0:T(8,128)}, bf16[128,4096]{1,0:T(8,128)(2,1)}, bf16[1024,4096]{1,0:T(8,128)(2,1)}) custom-call(bf16[1024,2048]{1,0:T(8,128)(2,1)} %get-tuple-element.55.refs_0_, bf16[1024,2048]{1,0:T(8,128)(2,1)} %get-tuple-element.58.refs_1_, bf16[2048,4096]{1,0:T(8,128)(2,1)} %refs_3_.1, ...), custom_call_target="tpu_custom_call" | custom-call | flops 68719476736 | bytes 67108864 | tf_op jit(solution)/shard_map/turn/pallas_call | solution.py:506
  376.5 0.1 reduce-scatter.14.cloned.1.call-start
  376.5 9.2 %dattn_out.2.refs_2_ = bf16[1024,512]{1,0:T(8,128)(2,1)} custom-call(bf16[1024,4096]{1,0:T(8,128)(2,1)} %get-tuple-element.65.refs_0_.refs_3_, bf16[512,4096]{1,0:T(8,128)(2,1)} %bitcast.29), custom_call_target="tpu_custom_call" | custom-call | flops 4294967296 | bytes 13631488 | tf_op jit(solution)/shard_map/dattn_out/pallas_call | solution.py:304
  385.7 30.7 %attn_bwd_1.1 = (bf16[1024,1536]{1,0:T(8,128)(2,1)}, f32[1024,512]{1,0:T(8,128)}, f32[1024,512]{1,0:T(8,128)}) custom-call(bf16[1024,1536]{1,0:T(8,128)(2,1)} %get-tuple-element.43.refs_0_, bf16[1024,1536]{1,0:T(8,128)(2,1)} %get-tuple-element.45.refs_1_, bf16[1024,512]{1,0:T(8,128)(2,1)} %dattn_out.2.refs_2_), custom_call_target="tpu_custom_call" | custom-call | flops 16106127360 | bytes 12582912 | tf_op jit(solution)/shard_map/attn_bwd_1/pallas_call | solution.py:145
  416.4 18.1 %qkv_back.2 = bf16[1024,4096]{1,0:T(8,128)(2,1)} custom-call(bf16[1024,1536]{1,0:T(8,128)(2,1)} %get-tuple-element.66.refs_0_.refs_3_, bf16[4096,1536]{1,0:T(8,128)(2,1)} %refs_1_.9), custom_call_target="tpu_custom_call" | custom-call | flops 12884901888 | bytes 24117248 | tf_op jit(solution)/shard_map/qkv_back/pallas_call | solution.py:304
  434.5 0.1 reduce-scatter.12.cloned.1.call-start
  434.6 9.2 %dattn_out.3.refs_1_ = bf16[1024,512]{1,0:T(8,128)(2,1)} custom-call(bf16[1024,4096]{1,0:T(8,128)(2,1)} %all-gather.6.cloned.1.call-done.refs_0_.refs_2_, bf16[512,4096]{1,0:T(8,128)(2,1)} %bitcast.30), custom_call_target="tpu_custom_call" | custom-call | flops 4294967296 | bytes 13631488 | tf_op jit(solution)/shard_map/dattn_out/pallas_call | solution.py:304
  443.9 15.4 %attn_bwd_0.1.refs_0_.refs_2_ = bf16[1024,1536]{1,0:T(8,128)(2,1)} custom-call(bf16[1024,1536]{1,0:T(8,128)(2,1)} %get-tuple-element.43.refs_0_, bf16[1024,512]{1,0:T(8,128)(2,1)} %dattn_out.3.refs_1_, f32[1024,512]{1,0:T(8,128)} %get-tuple-element.68.refs_2_, f32[1024,512]{1,0:T(8,128)} %get-tuple-element.69.refs_3_), custom_call_target="tpu_custom_call" | custom-call | flops 5368709120 | bytes 8388608 | tf_op jit(solution)/shard_map/attn_bwd_0/pallas_call | solution.py:145
  459.3 18.0 %qkv_back.3 = bf16[1024,4096]{1,0:T(8,128)(2,1)} custom-call(bf16[1024,1536]{1,0:T(8,128)(2,1)} %attn_bwd_0.1.refs_0_.refs_2_, bf16[4096,1536]{1,0:T(8,128)(2,1)} %refs_1_.9), custom_call_target="tpu_custom_call" | custom-call | flops 12884901888 | bytes 24117248 | tf_op jit(solution)/shard_map/qkv_back/pallas_call | solution.py:304
  477.3 0.1 all-gather.8.cloned.1.call-start
  477.4 0.8 dynamic-slice_bitcast_fusion
  478.2 0.7 copy.18.mu
  479.0 0.7 copy.19.rs
  479.7 0.7 copy.20.mu
  480.4 0.7 copy.21.rs
  481.1 33.0 %dwqkv.1 = bf16[4096,1536]{1,0:T(8,128)(2,1)} custom-call(bf16[1024,4096]{1,0:T(8,128)(2,1)} %get-tuple-element.70.refs_0_, bf16[1024,4096]{1,0:T(8,128)(2,1)} %get-tuple-element.71.refs_1_, bf16[1024,1536]{1,0:T(8,128)(2,1)} %attn_bwd_0.1.refs_0_.refs_2_, bf16[1024,1536]{1,0:T(8,128)(2,1)} %get-tuple-element.66.refs_0_.refs_3_), custom_call_target="tpu_custom_call" | custom-call | flops 25769803776 | bytes 35651584 | tf_op jit(solution)/shard_map/dwqkv/pallas_call | solution.py:304
  514.1 4.6 dx.2.refs_0_
  518.7 13.6 %dwo.1 = bf16[512,4096]{1,0:T(8,128)(2,1)} custom-call(bf16[1024,512]{1,0:T(8,128)(2,1)} %attn_fwd_0.1.refs_0_, bf16[1024,512]{1,0:T(8,128)(2,1)} %attn_fwd_1.1.refs_0_.refs_1_, bf16[1024,4096]{1,0:T(8,128)(2,1)} %all-gather.6.cloned.1.call-done.refs_0_.refs_2_, bf16[1024,4096]{1,0:T(8,128)(2,1)} %get-tuple-element.65.refs_0_.refs_3_), custom_call_target="tpu_custom_call" | custom-call | flops 8589934592 | bytes 23068672 | tf_op jit(solution)/shard_map/dwo/pallas_call | solution.py:304
  532.3 0.6 reduce-scatter.12.cloned.1.call-done.red
  532.9 4.6 dx.3
  537.5 41.4 %dw1.1 = bf16[4096,2048]{1,0:T(8,128)(2,1)} custom-call(bf16[1024,4096]{1,0:T(8,128)(2,1)} %get-tuple-element.53.n2_ref.refs_0_, bf16[1024,4096]{1,0:T(8,128)(2,1)} %all-gather.4.cloned.1.call-done.n2_ref.refs_1_, bf16[1024,2048]{1,0:T(8,128)(2,1)} %get-tuple-element.56.refs_0_.refs_2_, bf16[1024,2048]{1,0:T(8,128)(2,1)} %get-tuple-element.78.refs_0_.refs_3_), custom_call_target="tpu_custom_call" | custom-call | flops 34359738368 | bytes 41943040 | tf_op jit(solution)/shard_map/dw1/pallas_call | solution.py:304
  579.0 13.8 %relay.1 = bf16[2048,4096]{1,0:T(8,128)(2,1)} custom-call(bf16[2048,4096]{1,0:T(8,128)(2,1)} %get-tuple-element.80.i), custom_call_target="tpu_custom_call" | custom-call | flops 34359738368 | bytes 8388608 | tf_op jit(solution)/shard_map/relay/pallas_call | solution.py:556
  592.7 26.5 %all-gather.8.cloned.1.call-done = bf16[2,1024,4096]{2,1,0:T(8,128)(2,1)} async-done(((bf16[2,128,4096]{2,1,0:T(8,128)(2,1)}), bf16[2,1024,4096]{2,1,0:T(8,128)(2,1)}) %all-gather.8.cloned.1.call-update) | async-done | bytes 16777232 | tf_op jit(solution)/shard_map/all_gather | solution.py:637
  619.3 14.1 %copy.26 = bf16[2048,4096]{1,0:T(8,128)(2,1)} copy(bf16[2048,4096]{1,0:T(8,128)(2,1)} %bitcast.15) | data formatting | bytes 33554432
  (15 shorter events, 0.6 us)
Async XLA Ops:
  7.2 90.8 %reduce-scatter.6.cloned.1.call-start = ((), (), s32[]{:S(2)}) async-start(), calls=%async_computation.5 | async-start | bytes 9437184 | tf_op jit(solution)/shard_map/reduce_scatter | solution.py:579
  47.0 135.8 %reduce-scatter.8.cloned.1.call-start = ((), (), s32[]{:S(2)}) async-start(), calls=%async_computation.6 | async-start | bytes 9437184 | tf_op jit(solution)/shard_map/reduce_scatter | solution.py:579
  82.7 9.1 %copy-start = (bf16[4096]{0:T(1024)(128)(2,1)S(1)}, bf16[4096]{0:T(1024)(128)(2,1)}, u32[]{:S(2)}) copy-start(bf16[4096]{0:T(1024)(128)(2,1)} %param.14) | copy-start | bytes 24580
  91.5 141.9 %all-gather.4.cloned.1.call-start = ((), (), s32[]{:S(2)}) async-start(), calls=%async_computation.7 | async-start | bytes 9437184 | tf_op jit(solution)/shard_map/all_gather | solution.py:582
  187.3 97.2 %reduce-scatter.10.cloned.1.call-start = ((), (), s32[]{:S(2)}) async-start(), calls=%async_computation.8 | async-start | bytes 9437184 | tf_op jit(solution)/shard_map/reduce_scatter | solution.py:579
  226.4 208.3 %all-gather.6.cloned.1.call-start = ((), (), s32[]{:S(2)}) async-start(), calls=%async_computation.9 | async-start | bytes 9437184 | tf_op jit(solution)/shard_map/all_gather | solution.py:582
  376.5 137.7 %reduce-scatter.14.cloned.1.call-start = ((), (), s32[]{:S(2)}) async-start(), calls=%async_computation.11 | async-start | bytes 9437184 | tf_op jit(solution)/shard_map/reduce_scatter | solution.py:579
  434.5 98.4 %reduce-scatter.12.cloned.1.call-start = ((), (), s32[]{:S(2)}) async-start(), calls=%async_computation.10 | async-start | bytes 9437184 | tf_op jit(solution)/shard_map/reduce_scatter | solution.py:579
  477.3 142.0 %all-gather.8.cloned.1.call-start = ((), (), s32[]{:S(2)}) async-start(), calls=%async_computation.12 | async-start | bytes 18874368 | tf_op jit(solution)/shard_map/all_gather | solution.py:637
Sparse Core Ops, SparseCore 0:
  47.1 50.8 reduce-scatter.5
  100.9 81.8 reduce-scatter.7
  187.4 45.9 all-gather.3
  236.1 47.7 reduce-scatter.9
  376.6 45.0 all-gather.5
  434.7 47.2 reduce-scatter.13
  484.8 48.0 reduce-scatter.11
  537.7 81.5 all-gather.7
